TPU v7x, 8 devices: a whole 2x2x1 slice. The times are simulated.
8 devices in a mesh: dp: 2 (over z, y), pp: 4 (over x, core).
Axes of the slice: x: 2, y: 2, z: 1, core: 2. Of those that a mesh axis runs over, the one named last changes fastest.
Arguments:
- x_in: bfloat16 [8, 2, 1024, 768], P(('dp', 'pp')), parts along dimension 0
- dy_out: bfloat16 [8, 2, 1024, 768], P(('dp', 'pp')), parts along dimension 0
- w_qkv: bfloat16 [4, 2, 1, 768, 3, 12, 64], P('pp')
- w_attn: bfloat16 [4, 2, 1, 12, 64, 768], P('pp')
- w_fc: bfloat16 [4, 2, 1, 768, 3072], P('pp')
- w_proj: bfloat16 [4, 2, 1, 3072, 768], P('pp')
- b_qkv: bfloat16 [4, 2, 1, 3, 12, 64], P('pp')
- b_fc: bfloat16 [4, 2, 1, 3072], P('pp')
- vec_d: bfloat16 [4, 2, 1, 6, 768], P('pp')
Outputs:
- output 1: bfloat16 [8, 2, 1024, 768], P(('dp', 'pp')), parts along dimension 0
- output 2: bfloat16 [8, 2, 1024, 768], P(('dp', 'pp')), parts along dimension 0
- output 3: float32 [8, 2, 1, 768, 3, 12, 64], P(('dp', 'pp')), parts along dimension 0
- output 4: float32 [8, 2, 1, 12, 64, 768], P(('dp', 'pp')), parts along dimension 0
- output 5: float32 [8, 2, 1, 768, 3072], P(('dp', 'pp')), parts along dimension 0
- output 6: float32 [8, 2, 1, 3072, 768], P(('dp', 'pp')), parts along dimension 0
- output 7: float32 [8, 2, 1, 3, 12, 64], P(('dp', 'pp')), parts along dimension 0
- output 8: float32 [8, 2, 1, 3072], P(('dp', 'pp')), parts along dimension 0
- output 9: float32 [8, 2, 1, 6, 768], P(('dp', 'pp')), parts along dimension 0
There are 2 independent parts. A program takes and returns all parts, laid end to end along the dimension named above; an argument that names none is the same for every part.
All inputs are finite; a program needn't handle non-finite values.
Results may differ from a plain program's by a relative error of at most 0.0149549.
Values are sent between devices in bfloat16 or wider.
A program may use at most 1 GiB of HBM per device.

v0:
```python
import jax
import jax.numpy as jnp
from jax import lax
from jax.sharding import PartitionSpec as P

EPSILON = 1e-5


def layer_norm(rows_in, ln_gain, ln_shift):
    rows_f32 = rows_in.astype(jnp.float32)
    row_mean = jnp.mean(rows_f32, axis=-1, keepdims=True)
    centered = rows_f32 - row_mean
    row_var = jnp.mean(centered * centered, axis=-1, keepdims=True)
    scaled = centered * lax.rsqrt(row_var + EPSILON)
    return (scaled * ln_gain.astype(jnp.float32) + ln_shift.astype(jnp.float32)).astype(jnp.bfloat16)


def gpt_layer(hidden_in, layer_w):
    w_qkv, w_attn, w_fc, w_proj, b_qkv, b_fc, vec_d = layer_w
    n_batch, seq_len, d_model = hidden_in.shape
    n_heads, head_dim = w_qkv.shape[-2], w_qkv.shape[-1]
    tokens = n_batch * seq_len
    flat_rows = hidden_in.reshape(tokens, d_model)
    normed = layer_norm(flat_rows, vec_d[0], vec_d[1])
    qkv_proj = jnp.dot(normed, w_qkv.reshape(d_model, 3 * d_model), preferred_element_type=jnp.float32)
    qkv_proj = (qkv_proj + b_qkv.reshape(3 * d_model).astype(jnp.float32)).astype(jnp.bfloat16)
    qkv_proj = qkv_proj.reshape(n_batch, seq_len, 3, n_heads, head_dim)
    query_heads = qkv_proj[:, :, 0]
    key_heads = qkv_proj[:, :, 1]
    value_heads = qkv_proj[:, :, 2]
    scores = jnp.einsum('bqhe,bkhe->bhqk', query_heads, key_heads, preferred_element_type=jnp.float32) * (head_dim ** -0.5)
    causal = lax.broadcasted_iota(jnp.int32, (seq_len, seq_len), 0) >= lax.broadcasted_iota(jnp.int32, (seq_len, seq_len), 1)
    scores = jnp.where(causal, scores, -1e30)
    attn_probs = jax.nn.softmax(scores, axis=-1).astype(jnp.bfloat16)
    mixed_heads = jnp.einsum('bhqk,bkhe->bqhe', attn_probs, value_heads, preferred_element_type=jnp.float32).astype(jnp.bfloat16)
    attn_out = jnp.dot(mixed_heads.reshape(tokens, d_model), w_attn.reshape(d_model, d_model), preferred_element_type=jnp.float32)
    residual = (flat_rows.astype(jnp.float32) + attn_out + vec_d[2].astype(jnp.float32)).astype(jnp.bfloat16)
    normed_two = layer_norm(residual, vec_d[3], vec_d[4])
    hidden = jnp.dot(normed_two, w_fc, preferred_element_type=jnp.float32) + b_fc.astype(jnp.float32)
    hidden = jax.nn.gelu(hidden, approximate=True).astype(jnp.bfloat16)
    mlp_out = jnp.dot(hidden, w_proj, preferred_element_type=jnp.float32) + vec_d[5].astype(jnp.float32)
    return (residual.astype(jnp.float32) + mlp_out).astype(jnp.bfloat16).reshape(n_batch, seq_len, d_model)


def stage_forward(hidden_in, stage_w):
    for layer_idx in range(stage_w[0].shape[0]):
        hidden_in = gpt_layer(hidden_in, tuple(t[layer_idx] for t in stage_w))
    return hidden_in


def skip_forward(hidden_in, stage_w):
    return jnp.zeros_like(hidden_in)


def stage_backward(hidden_in, cotangent, stage_w, grad_acc):
    _, pull_back = jax.vjp(stage_forward, hidden_in, stage_w)
    d_input, d_weights = pull_back(cotangent)
    return d_input, tuple(a + g.astype(jnp.float32) for a, g in zip(grad_acc, d_weights))


def skip_backward(hidden_in, cotangent, stage_w, grad_acc):
    return jnp.zeros_like(hidden_in), grad_acc


def pick_row(buffer, index):
    return lax.dynamic_index_in_dim(buffer, index, 0, keepdims=False)


def store_row(buffer, row_val, index):
    return lax.dynamic_update_index_in_dim(buffer, row_val, index, 0)


def solution(mesh):
    n_stages = mesh.shape['pp']
    last = n_stages - 1
    to_next = [(i, i + 1) for i in range(last)]
    to_prev = [(i + 1, i) for i in range(last)]
    opposite = [(i, last - i) for i in range(n_stages)]
    data_spec = P(('dp', 'pp'))
    weight_spec = P('pp')

    def per_device(x_loc, dy_loc, *weights):
        dev_pos = lax.axis_index('pp')
        down_w = tuple(t[0, 0] for t in weights)
        up_w = tuple(t[0, 1] for t in weights)
        x_all = lax.all_gather(x_loc, 'pp', tiled=True)
        dy_all = lax.all_gather(dy_loc, 'pp', tiled=True)
        n_micro = x_all.shape[0]
        half_micro = n_micro // 2
        n_steps = half_micro + last
        act_shape = x_loc.shape[1:]
        zero_act = jnp.zeros(act_shape, x_loc.dtype)
        stash_zero = jnp.zeros((half_micro + 1,) + act_shape, x_loc.dtype)
        out_zero = jnp.zeros((n_micro + 1,) + act_shape, x_loc.dtype)

        def forward_step(step, carry):
            down_in, up_in, down_stash, up_stash, y_buf = carry
            down_idx = step - dev_pos
            up_idx = step - (last - dev_pos)
            down_ok = (down_idx >= 0) & (down_idx < half_micro)
            up_ok = (up_idx >= 0) & (up_idx < half_micro)
            down_row = jnp.clip(down_idx, 0, half_micro - 1)
            up_row = jnp.clip(up_idx, 0, half_micro - 1)
            down_act = jnp.where(dev_pos == 0, pick_row(x_all, down_row), down_in)
            up_act = jnp.where(dev_pos == last, pick_row(x_all, half_micro + up_row), up_in)
            down_stash = store_row(down_stash, down_act, jnp.where(down_ok, down_idx, half_micro))
            up_stash = store_row(up_stash, up_act, jnp.where(up_ok, up_idx, half_micro))
            down_out = lax.cond(down_ok, stage_forward, skip_forward, down_act, down_w)
            up_out = lax.cond(up_ok, stage_forward, skip_forward, up_act, up_w)
            y_buf = store_row(y_buf, down_out, jnp.where(down_ok & (dev_pos == last), down_idx, n_micro))
            y_buf = store_row(y_buf, up_out, jnp.where(up_ok & (dev_pos == 0), half_micro + up_idx, n_micro))
            down_in = lax.ppermute(down_out, 'pp', to_next)
            up_in = lax.ppermute(up_out, 'pp', to_prev)
            return down_in, up_in, down_stash, up_stash, y_buf

        fwd_init = (zero_act, zero_act, stash_zero, stash_zero, out_zero)
        _, _, down_stash, up_stash, y_buf = lax.fori_loop(0, n_steps, forward_step, fwd_init)
        y_loc = lax.psum_scatter(y_buf[:n_micro], 'pp', scatter_dimension=0, tiled=True)
        grad_zero = tuple(jnp.zeros(t.shape, jnp.float32) for t in down_w)

        def backward_step(step, carry):
            down_cot_in, up_cot_in, down_acc, up_acc, dx_buf = carry
            down_idx = step - (last - dev_pos)
            up_idx = step - dev_pos
            down_ok = (down_idx >= 0) & (down_idx < half_micro)
            up_ok = (up_idx >= 0) & (up_idx < half_micro)
            down_row = jnp.clip(down_idx, 0, half_micro - 1)
            up_row = jnp.clip(up_idx, 0, half_micro - 1)
            down_cot = jnp.where(dev_pos == last, pick_row(dy_all, down_row), down_cot_in)
            up_cot = jnp.where(dev_pos == 0, pick_row(dy_all, half_micro + up_row), up_cot_in)
            down_dx, down_acc = lax.cond(down_ok, stage_backward, skip_backward, pick_row(down_stash, down_row), down_cot, down_w, down_acc)
            up_dx, up_acc = lax.cond(up_ok, stage_backward, skip_backward, pick_row(up_stash, up_row), up_cot, up_w, up_acc)
            dx_buf = store_row(dx_buf, down_dx, jnp.where(down_ok & (dev_pos == 0), down_idx, n_micro))
            dx_buf = store_row(dx_buf, up_dx, jnp.where(up_ok & (dev_pos == last), half_micro + up_idx, n_micro))
            down_cot_in = lax.ppermute(down_dx, 'pp', to_prev)
            up_cot_in = lax.ppermute(up_dx, 'pp', to_next)
            return down_cot_in, up_cot_in, down_acc, up_acc, dx_buf

        bwd_init = (zero_act, zero_act, grad_zero, grad_zero, out_zero)
        _, _, down_acc, up_acc, dx_buf = lax.fori_loop(0, n_steps, backward_step, bwd_init)
        dx_loc = lax.psum_scatter(dx_buf[:n_micro], 'pp', scatter_dimension=0, tiled=True)
        peer_down = tuple(lax.ppermute(g, 'pp', opposite) for g in down_acc)
        peer_up = tuple(lax.ppermute(g, 'pp', opposite) for g in up_acc)
        grads = tuple(jnp.stack([mine_d + peer_u, mine_u + peer_d], axis=0)[None] for mine_d, mine_u, peer_d, peer_u in zip(down_acc, up_acc, peer_down, peer_up))
        return (y_loc, dx_loc) + grads

    return jax.shard_map(per_device, mesh=mesh, in_specs=(data_spec, data_spec) + (weight_spec,) * 7, out_specs=(data_spec, data_spec) + (data_spec,) * 7, check_vma=False)
```

profile of v0, /device:TPU:0, one launch (start us, length us, event | category | flops | bytes accessed | tf_op | source)
XLA Modules:
  0.0 7195.2 jit_solution(5468805996416702595)
XLA Ops:
  34.8 57.5 all-gather.3.cloned.1.call-done
  110.0 1461.0 %while.70 = (s32[]{:T(128)}, bf16[2,1024,768]{2,1,0:T(8,128)(2,1)}, bf16[2,1024,768]{2,1,0:T(8,128)(2,1)S(1)}, bf16[3,2,1024,768]{3,2,1,0:T(8,128)(2,1)}, bf16[3...) while((s32[]{:T(128)}, bf16[2,1024,768]{2,1,0:T(8,128)(2,1)}, ...), condition=%wide.region_17.18_spmd, body=%wide.region_0.17_spmd.sunk | while | flops 71422730240 | bytes 862572032 | solution.py:117
  116.6 182.6 %conditional.8 = (bf16[2,1024,768]{2,1,0:T(8,128)(2,1)}, bf16[1,2,1024,768]{3,2,1,0:T(8,128)(2,1)}) conditional(s32[]{:T(128)} %convert_element_type.1784, () %tuple.216, (bf16[2,1024,768]{2,1,0:T(8,128)(2,1)S(1)}, bf16[1,1,1,6,768]{4,3,2,1,0:T(8,128)(2,1)}, bf16[1,1,1,768,3,12,64]{3,6,5,4,2,1,0:T(8,128)(2,1)}, ...), branch_computations={%region_1.1_spmd, %region_2.8_spmd} | conditional | flops 35709792256 | bytes 392709952 | solution.py:108
  178.5 45.3 fusion.295
  323.6 182.7 %conditional.8 = (bf16[2,1024,768]{2,1,0:T(8,128)(2,1)}, bf16[1,2,1024,768]{3,2,1,0:T(8,128)(2,1)}) conditional(s32[]{:T(128)} %convert_element_type.1784, () %tuple.216, (bf16[2,1024,768]{2,1,0:T(8,128)(2,1)S(1)}, bf16[1,1,1,6,768]{4,3,2,1,0:T(8,128)(2,1)}, bf16[1,1,1,768,3,12,64]{3,6,5,4,2,1,0:T(8,128)(2,1)}, ...), branch_computations={%region_1.1_spmd, %region_2.8_spmd} | conditional | flops 35709792256 | bytes 392709952 | solution.py:108
  385.6 45.3 fusion.295
  538.5 210.3 %collective-permute-start = (bf16[2,1024,768]{2,1,0:T(8,128)(2,1)}, bf16[2,1024,768]{2,1,0:T(8,128)(2,1)}, u32[]{:S(2)}, u32[]{:S(2)}) collective-permute-start(bf16[2,1024,768]{2,1,0:T(8,128)(2,1)} %get-tuple-element.2613), channel_id=1, source_target_pairs={{0,1},{1,2},{2,3},{4,5},{5,6},{6,7}} | collective-permute-start | bytes 9437192 | tf_op jit(solution)/shard_map/while/body/eval_jaxpr/ppermute | solution.py:112
  763.0 167.1 %collective-permute-done.1 = bf16[2,1024,768]{2,1,0:T(8,128)(2,1)S(1)} collective-permute-done((bf16[2,1024,768]{2,1,0:T(8,128)(2,1)}, bf16[2,1024,768]{2,1,0:T(8,128)(2,1)S(1)}, u32[]{:S(2)}, u32[]{:S(2)}) %collective-permute-start.1) | collective-permute-done | bytes 3145760 | tf_op jit(solution)/shard_map/while/body/eval_jaxpr/ppermute | solution.py:113
  940.1 38.5 collective-permute-start
  978.7 174.2 %conditional.9 = (bf16[2,1024,768]{2,1,0:T(8,128)(2,1)}, bf16[1,2,1024,768]{3,2,1,0:T(8,128)(2,1)}) conditional(s32[]{:T(128)} %convert_element_type.1785, () %tuple.218, (bf16[2,1024,768]{2,1,0:T(8,128)(2,1)S(1)}, bf16[1,1,1,6,768]{4,3,2,1,0:T(8,128)(2,1)S(1)}, bf16[1,1,1,768,3,12,64]{3,6,5,4,2,1,0:T(8,128)(2,1)}, ...), branch_computations={%region_9.9_spmd, %region_10.16_spmd} | conditional | flops 35709792256 | bytes 394282816 | solution.py:109
  1033.1 45.3 fusion.297
  1161.7 172.4 %collective-permute-done.1 = bf16[2,1024,768]{2,1,0:T(8,128)(2,1)S(1)} collective-permute-done((bf16[2,1024,768]{2,1,0:T(8,128)(2,1)}, bf16[2,1024,768]{2,1,0:T(8,128)(2,1)S(1)}, u32[]{:S(2)}, u32[]{:S(2)}) %collective-permute-start.1) | collective-permute-done | bytes 3145760 | tf_op jit(solution)/shard_map/while/body/eval_jaxpr/ppermute | solution.py:113
  1347.0 35.7 collective-permute-start
  1382.7 174.5 %conditional.9 = (bf16[2,1024,768]{2,1,0:T(8,128)(2,1)}, bf16[1,2,1024,768]{3,2,1,0:T(8,128)(2,1)}) conditional(s32[]{:T(128)} %convert_element_type.1785, () %tuple.218, (bf16[2,1024,768]{2,1,0:T(8,128)(2,1)S(1)}, bf16[1,1,1,6,768]{4,3,2,1,0:T(8,128)(2,1)S(1)}, bf16[1,1,1,768,3,12,64]{3,6,5,4,2,1,0:T(8,128)(2,1)}, ...), branch_computations={%region_9.9_spmd, %region_10.16_spmd} | conditional | flops 35709792256 | bytes 394282816 | solution.py:109
  1437.4 45.3 fusion.297
  1624.7 3660.8 %while.71 = (s32[]{:T(128)}, bf16[2,1024,768]{2,1,0:T(8,128)(2,1)}, bf16[2,1024,768]{2,1,0:T(8,128)(2,1)}, f32[1,768,3,12,64]{1,4,3,2,0:T(8,128)}, f32[1,12,64,7...) while((s32[]{:T(128)}, bf16[2,1024,768]{2,1,0:T(8,128)(2,1)}, ...), condition=%wide.region_62.63_spmd, body=%wide.region_19.62_spmd.sunk | while | flops 195270311936 | bytes 3306145536 | solution.py:140
  1637.9 574.6 %conditional.11 = (bf16[2,1024,768]{2,1,0:T(8,128)(2,1)}, f32[1,768,3,12,64]{1,4,3,2,0:T(8,128)}, f32[1,12,64,768]{3,2,1,0:T(8,128)}, f32[1,768,3072]{2,1,0:T(8,...) conditional(s32[]{:T(128)} %convert_element_type.1787, ...), branch_computations={%region_41.41_spmd, %region_42.61_spmd} | conditional | flops 97635155968 | bytes 1634987648 | solution.py:132
  1706.3 46.4 fusion.304
  1753.5 48.5 divide_convert_fusion.9
  1979.7 49.3 fusion.204
  2029.1 52.9 convert_bitcast_fusion.6
  2082.0 51.2 convert_bitcast_fusion.7
  2236.9 574.4 %conditional.11 = (bf16[2,1024,768]{2,1,0:T(8,128)(2,1)}, f32[1,768,3,12,64]{1,4,3,2,0:T(8,128)}, f32[1,12,64,768]{3,2,1,0:T(8,128)}, f32[1,768,3072]{2,1,0:T(8,...) conditional(s32[]{:T(128)} %convert_element_type.1787, ...), branch_computations={%region_41.41_spmd, %region_42.61_spmd} | conditional | flops 97635155968 | bytes 1634987648 | solution.py:132
  2304.9 46.4 fusion.304
  2352.1 48.5 divide_convert_fusion.9
  2578.4 49.3 fusion.204
  2627.8 53.1 convert_bitcast_fusion.6
  2680.8 51.2 convert_bitcast_fusion.7
  2846.3 1164.1 %collective-permute-start.3 = (bf16[2,1024,768]{2,1,0:T(8,128)(2,1)}, bf16[2,1024,768]{2,1,0:T(8,128)(2,1)S(1)}, u32[]{:S(2)}, u32[]{:S(2)}) collective-permute-start(bf16[2,1024,768]{2,1,0:T(8,128)(2,1)} %get-tuple-element.2660), channel_id=1, source_target_pairs={{0,1},{1,2},{2,3},{4,5},{5,6},{6,7}} | collective-permute-start | bytes 9437192 | tf_op jit(solution)/shard_map/while/body/eval_jaxpr/ppermute | solution.py:136
  4020.0 579.9 %conditional.10 = (bf16[2,1024,768]{2,1,0:T(8,128)(2,1)}, f32[1,768,3,12,64]{1,4,3,2,0:T(8,128)}, f32[1,12,64,768]{3,2,1,0:T(8,128)}, f32[1,768,3072]{2,1,0:T(8,...) conditional(s32[]{:T(128)} %convert_element_type.1786, ...), branch_computations={%region_20.20_spmd, %region_21.40_spmd} | conditional | flops 97635155968 | bytes 1620788864 | solution.py:131
  4093.6 46.4 fusion.300
  4140.7 48.5 divide_convert_fusion.8
  4367.0 49.3 fusion.116
  4416.4 52.9 convert_bitcast_fusion.2
  4469.3 51.2 convert_bitcast_fusion.3
  4650.5 579.6 %conditional.10 = (bf16[2,1024,768]{2,1,0:T(8,128)(2,1)}, f32[1,768,3,12,64]{1,4,3,2,0:T(8,128)}, f32[1,12,64,768]{3,2,1,0:T(8,128)}, f32[1,768,3072]{2,1,0:T(8,...) conditional(s32[]{:T(128)} %convert_element_type.1786, ...), branch_computations={%region_20.20_spmd, %region_21.40_spmd} | conditional | flops 97635155968 | bytes 1620788864 | solution.py:131
  4723.8 46.4 fusion.300
  4770.9 48.5 divide_convert_fusion.8
  4997.3 49.3 fusion.116
  5046.6 53.1 convert_bitcast_fusion.2
  5099.7 51.2 convert_bitcast_fusion.3
  5296.1 571.4 %collective-permute-start.5 = (f32[1,768,3,12,64]{1,4,3,2,0:T(8,128)}, f32[1,768,3,12,64]{1,4,3,2,0:T(8,128)S(1)}, u32[]{:S(2)}, u32[]{:S(2)}) collective-permute-start(f32[1,768,3,12,64]{1,4,3,2,0:T(8,128)} %get-tuple-element.1965), channel_id=1, source_target_pairs={{0,3},{1,2},{2,1},{3,0},{4,7},{5,6},{6,5},{7,4}} | collective-permute-start | bytes 21233672 | tf_op jit(solution)/shard_map/ppermute | solution.py:142
  5871.1 469.6 %collective-permute-done.12 = f32[1,3,12,64]{3,0,2,1:T(1,128)S(1)} collective-permute-done((f32[1,3,12,64]{3,0,2,1:T(1,128)S(1)}, f32[1,3,12,64]{3,0,2,1:T(1,128)S(1)}, u32[]{:S(2)}, u32[]{:S(2)}) %collective-permute-start.12) | collective-permute-done | bytes 9248 | tf_op jit(solution)/shard_map/ppermute | solution.py:143
  6347.0 152.4 %collective-permute-done.13 = f32[1,3,12,64]{3,0,2,1:T(1,128)S(1)} collective-permute-done((f32[1,3,12,64]{3,0,2,1:T(1,128)S(1)}, f32[1,3,12,64]{3,0,2,1:T(1,128)S(1)}, u32[]{:S(2)}, u32[]{:S(2)}) %collective-permute-start.13) | collective-permute-done | bytes 9248 | tf_op jit(solution)/shard_map/ppermute | solution.py:142
  6504.6 51.6 collective-permute-done.6
  6608.8 149.6 %collective-permute-done.8 = f32[1,768,3072]{2,1,0:T(8,128)} collective-permute-done((f32[1,768,3072]{2,1,0:T(8,128)}, f32[1,768,3072]{2,1,0:T(8,128)}, u32[]{:S(2)}, u32[]{:S(2)}) %collective-permute-start.8) | collective-permute-done | bytes 9437216 | tf_op jit(solution)/shard_map/ppermute | solution.py:143
  6784.3 176.3 %collective-permute-done.11 = f32[1,3072,768]{2,1,0:T(8,128)} collective-permute-done((f32[1,3072,768]{2,1,0:T(8,128)}, f32[1,3072,768]{2,1,0:T(8,128)}, u32[]{:S(2)}, u32[]{:S(2)}) %collective-permute-start.11) | collective-permute-done | bytes 9437216 | tf_op jit(solution)/shard_map/ppermute | solution.py:142
  6971.9 190.7 %collective-permute-done.10 = f32[1,3072,768]{2,1,0:T(8,128)} collective-permute-done((f32[1,3072,768]{2,1,0:T(8,128)}, f32[1,3072,768]{2,1,0:T(8,128)}, u32[]{:S(2)}, u32[]{:S(2)}) %collective-permute-start.10) | collective-permute-done | bytes 9437216 | tf_op jit(solution)/shard_map/ppermute | solution.py:143
  (1018 shorter events, 2421.6 us)
Async XLA Ops:
  7.2 85.2 %all-gather.3.cloned.1.call-start = ((), (), s32[]{:S(2)}) async-start(), calls=%async_computation.2 | async-start | bytes 15728640 | tf_op jit(solution)/shard_map/all_gather | solution.py:86
  7.9 1573.7 %all-gather.5.cloned.1.call-start = ((), (), s32[]{:S(2)}) async-start(), calls=%async_computation.3 | async-start | bytes 15728640 | tf_op jit(solution)/shard_map/all_gather | solution.py:87
  8.7 7179.7 %reduce-scatter.7.cloned.1.call-start = ((), (), s32[]{:S(2)}) async-start(), calls=%async_computation.4 | async-start | bytes 15728640
  299.2 18.0 collective-permute-start
  308.4 8.9 collective-permute-start.1
  506.2 19.3 collective-permute-start
  516.7 8.9 collective-permute-start.1
  532.1 216.7 %copy-start.44 = (bf16[1,1,1,6,768]{4,3,2,1,0:T(8,128)(2,1)S(1)}, bf16[1,1,1,6,768]{4,3,2,1,0:T(8,128)(2,1)}, u32[]{:S(2)}) copy-start(bf16[1,1,1,6,768]{4,3,2,1,0:T(8,128)(2,1)} %get-tuple-element.2803) | copy-start | bytes 27652 | tf_op jit(solution)/shard_map/while
  532.1 216.7 %copy-start.58 = (bf16[1,1,1,3,12,64]{5,4,3,2,1,0:T(8,128)(2,1)S(1)}, bf16[1,1,1,3,12,64]{5,4,3,2,1,0:T(8,128)(2,1)}, u32[]{:S(2)}) copy-start(bf16[1,1,1,3,12,64]{5,4,3,2,1,0:T(8,128)(2,1)} %get-tuple-element.2805) | copy-start | bytes 13828 | tf_op jit(solution)/shard_map/while
  538.5 224.5 %collective-permute-start = (bf16[2,1024,768]{2,1,0:T(8,128)(2,1)}, bf16[2,1024,768]{2,1,0:T(8,128)(2,1)}, u32[]{:S(2)}, u32[]{:S(2)}) collective-permute-start(bf16[2,1024,768]{2,1,0:T(8,128)(2,1)} %get-tuple-element.2613), channel_id=1, source_target_pairs={{0,1},{1,2},{2,3},{4,5},{5,6},{6,7}} | collective-permute-start | bytes 9437192 | tf_op jit(solution)/shard_map/while/body/eval_jaxpr/ppermute | solution.py:112
  754.2 175.9 %collective-permute-start.1 = (bf16[2,1024,768]{2,1,0:T(8,128)(2,1)}, bf16[2,1024,768]{2,1,0:T(8,128)(2,1)S(1)}, u32[]{:S(2)}, u32[]{:S(2)}) collective-permute-start(bf16[2,1024,768]{2,1,0:T(8,128)(2,1)} %get-tuple-element.2615), channel_id=1, source_target_pairs={{1,0},{2,1},{3,2},{5,4},{6,5},{7,6}} | collective-permute-start | bytes 9437192 | tf_op jit(solution)/shard_map/while/body/eval_jaxpr/ppermute | solution.py:113
  940.1 221.6 %collective-permute-start = (bf16[2,1024,768]{2,1,0:T(8,128)(2,1)}, bf16[2,1024,768]{2,1,0:T(8,128)(2,1)}, u32[]{:S(2)}, u32[]{:S(2)}) collective-permute-start(bf16[2,1024,768]{2,1,0:T(8,128)(2,1)} %get-tuple-element.2613), channel_id=1, source_target_pairs={{0,1},{1,2},{2,3},{4,5},{5,6},{6,7}} | collective-permute-start | bytes 9437192 | tf_op jit(solution)/shard_map/while/body/eval_jaxpr/ppermute | solution.py:112
  1152.9 181.2 %collective-permute-start.1 = (bf16[2,1024,768]{2,1,0:T(8,128)(2,1)}, bf16[2,1024,768]{2,1,0:T(8,128)(2,1)S(1)}, u32[]{:S(2)}, u32[]{:S(2)}) collective-permute-start(bf16[2,1024,768]{2,1,0:T(8,128)(2,1)} %get-tuple-element.2615), channel_id=1, source_target_pairs={{1,0},{2,1},{3,2},{5,4},{6,5},{7,6}} | collective-permute-start | bytes 9437192 | tf_op jit(solution)/shard_map/while/body/eval_jaxpr/ppermute | solution.py:113
  1347.0 219.0 %collective-permute-start = (bf16[2,1024,768]{2,1,0:T(8,128)(2,1)}, bf16[2,1024,768]{2,1,0:T(8,128)(2,1)}, u32[]{:S(2)}, u32[]{:S(2)}) collective-permute-start(bf16[2,1024,768]{2,1,0:T(8,128)(2,1)} %get-tuple-element.2613), channel_id=1, source_target_pairs={{0,1},{1,2},{2,3},{4,5},{5,6},{6,7}} | collective-permute-start | bytes 9437192 | tf_op jit(solution)/shard_map/while/body/eval_jaxpr/ppermute | solution.py:112
  1557.2 8.9 collective-permute-start.1
  1581.5 5606.9 %reduce-scatter.9.cloned.1.call-start = ((), (), s32[]{:S(2)}) async-start(), calls=%async_computation.5 | async-start | bytes 15728640
  1636.6 585.0 %collective-permute-start.2 = (bf16[2,1024,768]{2,1,0:T(8,128)(2,1)}, bf16[2,1024,768]{2,1,0:T(8,128)(2,1)}, u32[]{:S(2)}, u32[]{:S(2)}) collective-permute-start(bf16[2,1024,768]{2,1,0:T(8,128)(2,1)} %get-tuple-element.2659), channel_id=1, source_target_pairs={{1,0},{2,1},{3,2},{5,4},{6,5},{7,6}} | collective-permute-start | bytes 9437192 | tf_op jit(solution)/shard_map/while/body/eval_jaxpr/ppermute | solution.py:135
  2212.6 9.1 collective-permute-start.3
  2235.6 587.1 %collective-permute-start.2 = (bf16[2,1024,768]{2,1,0:T(8,128)(2,1)}, bf16[2,1024,768]{2,1,0:T(8,128)(2,1)}, u32[]{:S(2)}, u32[]{:S(2)}) collective-permute-start(bf16[2,1024,768]{2,1,0:T(8,128)(2,1)} %get-tuple-element.2659), channel_id=1, source_target_pairs={{1,0},{2,1},{3,2},{5,4},{6,5},{7,6}} | collective-permute-start | bytes 9437192 | tf_op jit(solution)/shard_map/while/body/eval_jaxpr/ppermute | solution.py:135
  2811.3 11.4 collective-permute-start.3
  2836.6 1181.4 %collective-permute-start.2 = (bf16[2,1024,768]{2,1,0:T(8,128)(2,1)}, bf16[2,1024,768]{2,1,0:T(8,128)(2,1)}, u32[]{:S(2)}, u32[]{:S(2)}) collective-permute-start(bf16[2,1024,768]{2,1,0:T(8,128)(2,1)} %get-tuple-element.2659), channel_id=1, source_target_pairs={{1,0},{2,1},{3,2},{5,4},{6,5},{7,6}} | collective-permute-start | bytes 9437192 | tf_op jit(solution)/shard_map/while/body/eval_jaxpr/ppermute | solution.py:135
  2846.3 1171.7 %collective-permute-start.3 = (bf16[2,1024,768]{2,1,0:T(8,128)(2,1)}, bf16[2,1024,768]{2,1,0:T(8,128)(2,1)S(1)}, u32[]{:S(2)}, u32[]{:S(2)}) collective-permute-start(bf16[2,1024,768]{2,1,0:T(8,128)(2,1)} %get-tuple-element.2660), channel_id=1, source_target_pairs={{0,1},{1,2},{2,3},{4,5},{5,6},{6,7}} | collective-permute-start | bytes 9437192 | tf_op jit(solution)/shard_map/while/body/eval_jaxpr/ppermute | solution.py:136
  4020.0 581.2 %copy-start.45 = (bf16[1,1,1,6,768]{4,3,2,1,0:T(8,128)(2,1)S(1)}, bf16[1,1,1,6,768]{4,3,2,1,0:T(8,128)(2,1)}, u32[]{:S(2)}) copy-start(bf16[1,1,1,6,768]{4,3,2,1,0:T(8,128)(2,1)} %get-tuple-element.2938) | copy-start | bytes 27652 | tf_op jit(solution)/shard_map/while
  4599.9 48.5 collective-permute-start.2
  4609.6 38.8 collective-permute-start.3
  4650.5 580.9 %copy-start.45 = (bf16[1,1,1,6,768]{4,3,2,1,0:T(8,128)(2,1)S(1)}, bf16[1,1,1,6,768]{4,3,2,1,0:T(8,128)(2,1)}, u32[]{:S(2)}) copy-start(bf16[1,1,1,6,768]{4,3,2,1,0:T(8,128)(2,1)} %get-tuple-element.2938) | copy-start | bytes 27652 | tf_op jit(solution)/shard_map/while
  5230.1 46.7 collective-permute-start.2
  5240.1 36.7 collective-permute-start.3
  5296.0 573.2 %copy-start.80 = (f32[1,3072]{1,0:T(1,128)S(1)}, f32[1,3072]{1,0:T(1,128)}, u32[]{:S(2)}) copy-start(f32[1,3072]{1,0:T(1,128)} %get-tuple-element.1976) | copy-start | bytes 36868
  5296.0 573.2 %copy-start.57 = (f32[1,3,12,64]{3,2,1,0:T(8,128)S(1)}, f32[1,3,12,64]{3,2,1,0:T(8,128)}, u32[]{:S(2)}) copy-start(f32[1,3,12,64]{3,2,1,0:T(8,128)} %get-tuple-element.1974) | copy-start | bytes 27652
  5296.0 575.0 %copy-start.54 = (f32[1,6,768]{2,1,0:T(8,128)S(1)}, f32[1,6,768]{2,1,0:T(8,128)}, u32[]{:S(2)}) copy-start(f32[1,6,768]{2,1,0:T(8,128)} %get-tuple-element.1978) | copy-start | bytes 55300
  5296.0 1044.7 %copy-start.83 = (f32[1,3072]{1,0:T(1,128)S(1)}, f32[1,3072]{1,0:T(1,128)}, u32[]{:S(2)}) copy-start(f32[1,3072]{1,0:T(1,128)} %get-tuple-element.1975) | copy-start | bytes 36868
  5296.0 1047.0 %copy-start.67 = (f32[1,3,12,64]{3,2,1,0:T(8,128)S(1)}, f32[1,3,12,64]{3,2,1,0:T(8,128)}, u32[]{:S(2)}) copy-start(f32[1,3,12,64]{3,2,1,0:T(8,128)} %get-tuple-element.1973) | copy-start | bytes 27652
  5296.1 1050.9 %copy-start.64 = (f32[1,6,768]{2,1,0:T(8,128)S(1)}, f32[1,6,768]{2,1,0:T(8,128)}, u32[]{:S(2)}) copy-start(f32[1,6,768]{2,1,0:T(8,128)} %get-tuple-element.1977) | copy-start | bytes 55300
  5296.1 1262.4 %collective-permute-start.5 = (f32[1,768,3,12,64]{1,4,3,2,0:T(8,128)}, f32[1,768,3,12,64]{1,4,3,2,0:T(8,128)S(1)}, u32[]{:S(2)}, u32[]{:S(2)}) collective-permute-start(f32[1,768,3,12,64]{1,4,3,2,0:T(8,128)} %get-tuple-element.1965), channel_id=1, source_target_pairs={{0,3},{1,2},{2,1},{3,0},{4,7},{5,6},{6,5},{7,4}} | collective-permute-start | bytes 21233672 | tf_op jit(solution)/shard_map/ppermute | solution.py:142
  5867.5 637.0 %collective-permute-start.7 = (f32[1,12,64,768]{3,2,1,0:T(8,128)}, f32[1,12,64,768]{3,2,1,0:T(8,128)S(1)}, u32[]{:S(2)}, u32[]{:S(2)}) collective-permute-start(f32[1,12,64,768]{3,2,1,0:T(8,128)} %get-tuple-element.1967), channel_id=1, source_target_pairs={{0,3},{1,2},{2,1},{3,0},{4,7},{5,6},{6,5},{7,4}} | collective-permute-start | bytes 7077896 | tf_op jit(solution)/shard_map/ppermute | solution.py:142
  5867.5 728.4 %collective-permute-start.9 = (f32[1,768,3072]{2,1,0:T(8,128)}, f32[1,768,3072]{2,1,0:T(8,128)}, u32[]{:S(2)}, u32[]{:S(2)}) collective-permute-start(f32[1,768,3072]{2,1,0:T(8,128)} %get-tuple-element.1969), channel_id=1, source_target_pairs={{0,3},{1,2},{2,1},{3,0},{4,7},{5,6},{6,5},{7,4}} | collective-permute-start | bytes 28311560 | tf_op jit(solution)/shard_map/ppermute | solution.py:142
  5869.2 473.8 %collective-permute-start.14 = (f32[1,3072]{1,0:T(1,128)S(1)}, f32[1,3072]{1,0:T(1,128)S(1)}, u32[]{:S(2)}, u32[]{:S(2)}) collective-permute-start(f32[1,3072]{1,0:T(1,128)S(1)} %copy-done.80), channel_id=1, source_target_pairs={{0,3},{1,2},{2,1},{3,0},{4,7},{5,6},{6,5},{7,4}} | collective-permute-start | bytes 36872 | tf_op jit(solution)/shard_map/ppermute | solution.py:143
  5869.3 471.4 %collective-permute-start.12 = (f32[1,3,12,64]{3,0,2,1:T(1,128)S(1)}, f32[1,3,12,64]{3,0,2,1:T(1,128)S(1)}, u32[]{:S(2)}, u32[]{:S(2)}) collective-permute-start(f32[1,3,12,64]{3,0,2,1:T(1,128)S(1)} %copy.162), channel_id=1, source_target_pairs={{0,3},{1,2},{2,1},{3,0},{4,7},{5,6},{6,5},{7,4}} | collective-permute-start | bytes 27656 | tf_op jit(solution)/shard_map/ppermute | solution.py:143
  6340.7 3.7 collective-permute-start.15
  6343.0 3.5 collective-permute-start.16
  6344.4 232.4 %collective-permute-start.4 = (f32[1,768,3,12,64]{1,4,3,2,0:T(8,128)}, f32[1,768,3,12,64]{1,4,3,2,0:T(8,128)}, u32[]{:S(2)}, u32[]{:S(2)}) collective-permute-start(f32[1,768,3,12,64]{1,4,3,2,0:T(8,128)} %get-tuple-element.1966), channel_id=1, source_target_pairs={{0,3},{1,2},{2,1},{3,0},{4,7},{5,6},{6,5},{7,4}} | collective-permute-start | bytes 21233672 | tf_op jit(solution)/shard_map/ppermute | solution.py:143
  6346.6 152.8 %collective-permute-start.13 = (f32[1,3,12,64]{3,0,2,1:T(1,128)S(1)}, f32[1,3,12,64]{3,0,2,1:T(1,128)S(1)}, u32[]{:S(2)}, u32[]{:S(2)}) collective-permute-start(f32[1,3,12,64]{3,0,2,1:T(1,128)S(1)} %get-tuple-element.2156), channel_id=1, source_target_pairs={{0,3},{1,2},{2,1},{3,0},{4,7},{5,6},{6,5},{7,4}} | collective-permute-start | bytes 27656 | tf_op jit(solution)/shard_map/ppermute | solution.py:142
  6499.4 3.4 collective-permute-start.17
  6502.8 53.3 collective-permute-start.6
  6504.5 253.9 %collective-permute-start.8 = (f32[1,768,3072]{2,1,0:T(8,128)}, f32[1,768,3072]{2,1,0:T(8,128)}, u32[]{:S(2)}, u32[]{:S(2)}) collective-permute-start(f32[1,768,3072]{2,1,0:T(8,128)} %get-tuple-element.1970), channel_id=1, source_target_pairs={{0,3},{1,2},{2,1},{3,0},{4,7},{5,6},{6,5},{7,4}} | collective-permute-start | bytes 28311560 | tf_op jit(solution)/shard_map/ppermute | solution.py:143
  6556.1 404.5 %collective-permute-start.11 = (f32[1,3072,768]{2,1,0:T(8,128)}, f32[1,3072,768]{2,1,0:T(8,128)}, u32[]{:S(2)}, u32[]{:S(2)}) collective-permute-start(f32[1,3072,768]{2,1,0:T(8,128)} %get-tuple-element.1971), channel_id=1, source_target_pairs={{0,3},{1,2},{2,1},{3,0},{4,7},{5,6},{6,5},{7,4}} | collective-permute-start | bytes 28311560 | tf_op jit(solution)/shard_map/ppermute | solution.py:142
  6558.5 604.0 %collective-permute-start.10 = (f32[1,3072,768]{2,1,0:T(8,128)}, f32[1,3072,768]{2,1,0:T(8,128)}, u32[]{:S(2)}, u32[]{:S(2)}) collective-permute-start(f32[1,3072,768]{2,1,0:T(8,128)} %get-tuple-element.1972), channel_id=1, source_target_pairs={{0,3},{1,2},{2,1},{3,0},{4,7},{5,6},{6,5},{7,4}} | collective-permute-start | bytes 28311560 | tf_op jit(solution)/shard_map/ppermute | solution.py:143
  (235 other events, 4833.4 us)
Sparse Core Ops, SparseCore 0:
  9.5 82.7 all-gather.2
  93.9 97.9 all-gather.4
  1581.6 105.4 reduce-scatter.6
  5296.2 730.1 reduce-scatter.8
where the time goes:
time: 7210 us; the launch traced here: 7200 us
  starting transfers between devices  2120 us (29%)
  matrix products  2020 us (28%)
  waiting for transfers between devices  1590 us (22%)
  local copies, waits for them, and re-layouts  800 us (11%)
  other arithmetic  573 us (8%)
    ppermute x5, starting transfers between devices, backward_step(): up_cot_in = lax.ppermute(up_dx, 'pp', to_next)  1230 us
    ppermute x7, waiting for transfers between devices, per_device(): peer_up = tuple((lax.ppermute(g, 'pp', opposite) for g in up_acc))  861 us
    ppermute x7, starting transfers between devices, per_device(): peer_down = tuple((lax.ppermute(g, 'pp', opposite) for g in down_acc))  580 us
    dot_general x16, matrix products, gpt_layer(): jnp.einsum('bhqk,bkhe->bqhe', attn_probs, value_heads, preferred_element_...  497 us
    dot_general x8, matrix products, gpt_layer(): jnp.einsum('bqhe,bkhe->bhqk', query_heads, key_heads, preferred_element_t...  417 us
    sub x8, matrix products, gpt_layer(): attn_probs = jax.nn.softmax(scores, axis=-1).astype(jnp.bfloat16)  367 us
    ppermute x5, waiting for transfers between devices, forward_step(): up_in = lax.ppermute(up_out, 'pp', to_prev)  339 us
    ppermute x7, waiting for transfers between devices, per_device(): peer_down = tuple((lax.ppermute(g, 'pp', opposite) for g in down_acc))  332 us
  transfers between devices with their start and end apart: 38, of which 11 were waited for; matrix products, arithmetic and copies ran while one was open for 47% of the time, Pallas kernels for 0%

commit v1 on v0

v1 whole, which is shorter than its diff:
```python
import functools

import jax
import jax.numpy as jnp
from jax import lax
from jax.experimental import pallas as pl
from jax.experimental.pallas import tpu as pltpu
from jax.sharding import PartitionSpec as P

EPSILON = 1e-5
HEADS = 12
HEAD = 64
LANES = 128
WIDTH = HEADS * HEAD
PAIRS = WIDTH // LANES
LOG2E = 1.4426950408889634
SCALE = HEAD ** -0.5
EXP_SCALE = SCALE * LOG2E
BLK = 256
ROWS = 512
HALF = WIDTH // 2
FOUR = 4
N_STAT = 16
GELU_C = 0.7978845608028654
GELU_A = 0.044715
GELU_CA = GELU_C * GELU_A
ROW_FC, ROW_G1, ROW_S1, ROW_BO, ROW_G2, ROW_S2, ROW_B2 = 3, 7, 8, 9, 10, 11, 12
VMEM_LIMIT = 60 * 1024 * 1024
F32 = jnp.float32
BF16 = jnp.bfloat16
NT = (((1,), (1,)), ((), ()))
NN = (((1,), (0,)), ((), ()))
TN = (((0,), (0,)), ((), ()))
ANY = pl.BlockSpec(memory_space=pl.ANY)
MESH_ID = pl.DeviceIdType.MESH


def mm(a, b, dims):
    return lax.dot_general(a, b, dims, preferred_element_type=F32)


def iota(shape, dim):
    return lax.broadcasted_iota(jnp.int32, shape, dim)


def row_max(x):
    return jnp.max(x, axis=-1, keepdims=True)


def row_sum(x):
    return jnp.sum(x, axis=-1, keepdims=True)


def col_sum(x):
    return jnp.sum(x, axis=0, keepdims=True)


def row_mean(x):
    return jnp.mean(x, axis=-1, keepdims=True)


def chunk(index):
    return slice(index * WIDTH, (index + 1) * WIDTH)


def lanes_of(index):
    return pl.ds(pl.multiple_of(index * LANES, LANES), LANES)


def rows_of(index):
    return pl.ds(pl.multiple_of(index * ROWS, ROWS), ROWS)


def stat_row(s_ref, row):
    return s_ref[0, row : row + 1]


def ln_parts(rows_in):
    rows = rows_in.astype(F32)
    centered = rows - row_mean(rows)
    inv = lax.rsqrt(row_mean(centered * centered) + EPSILON)
    return centered * inv, inv


def ln_apply(rows_in, gain, shift):
    scaled, _ = ln_parts(rows_in)
    return (scaled * gain + shift).astype(BF16)


def ln_grad(rows_in, gain, d_out):
    scaled, inv = ln_parts(rows_in)
    d_scaled = d_out * gain
    d_rows = (inv * (d_scaled - row_mean(d_scaled) - scaled * row_mean(d_scaled * scaled))).astype(BF16)
    return d_rows, col_sum(d_out * scaled), col_sum(d_out)


def gelu_terms(pre):
    square = pre * pre
    t = jnp.tanh(pre * (GELU_C + GELU_CA * square))
    return square, t, 0.5 + 0.5 * t


def start_load(flags_ref, layer, pair, dst, sem):
    own_ref, peer_ref = pair

    @pl.when(flags_ref[layer, 0] == 1)
    def _():
        pltpu.make_async_copy(own_ref.at[flags_ref[layer, 1]], dst, sem).start()

    @pl.when(flags_ref[layer, 0] == 0)
    def _():
        pltpu.make_async_copy(peer_ref.at[flags_ref[layer, 1]], dst, sem).start()


def wait_load(pair, dst, sem):
    pltpu.make_async_copy(pair[0].at[0], dst, sem).wait()


def attend(qkv_ref, o_ref, lse_scr, pair, seq):
    lane = iota((BLK, LANES), 1)
    causal = iota((BLK, BLK), 0) >= iota((BLK, BLK), 1)
    q_at, k_at, v_at = (lanes_of(t * PAIRS + pair) for t in range(3))
    zero = jnp.zeros((BLK, LANES), BF16)
    for i in range(seq // BLK):
        past, rows = slice(0, i * BLK), slice(i * BLK, (i + 1) * BLK)
        q_blk = qkv_ref[rows, q_at]
        heads_out = []
        stats = lse_scr[rows, :]
        for h in range(2):
            q_h = jnp.where((lane < HEAD) == (h == 0), q_blk, zero)
            s_d = jnp.where(causal, mm(q_h, qkv_ref[rows, k_at], NT), -1e30)
            top = row_max(s_d)
            if i:
                s_o = mm(q_h, qkv_ref[past, k_at], NT)
                top = jnp.maximum(top, row_max(s_o))
            e_d = jnp.exp2((s_d - top) * EXP_SCALE)
            total = row_sum(e_d)
            if i:
                e_o = jnp.exp2((s_o - top) * EXP_SCALE)
                total = total + row_sum(e_o)
            inv = 1.0 / total
            out = mm((e_d * inv).astype(BF16), qkv_ref[rows, v_at], NN)
            if i:
                out = out + mm((e_o * inv).astype(BF16), qkv_ref[past, v_at], NN)
            heads_out.append(out)
            stats = jnp.where(lane == 2 * pair + h, top * EXP_SCALE + jnp.log2(total), stats)
        o_ref[rows, lanes_of(pair)] = jnp.where(lane < HEAD, *heads_out).astype(BF16)
        lse_scr[rows, :] = stats


def forward_body(keep_u, flags_ref, x_ref, s_ref, *refs):
    weights = [refs[2 * k : 2 * k + 2] for k in range(FOUR)]
    n_out = 7 + keep_u
    outs = refs[2 * FOUR : 2 * FOUR + n_out]
    w_bufs = refs[2 * FOUR + n_out : 3 * FOUR + n_out]
    h_scr, a_scr, qkv_scr, o_scr, lse_scr, lse_t, h1_scr, a2_scr, w_sems, out_sems, x_sem = refs[3 * FOUR + n_out : 3 * FOUR + n_out + 11]
    u_scr = refs[-1] if keep_u else None
    layer = pl.program_id(0)
    n_layers = pl.num_programs(0)
    slot = layer % 2
    seq = x_ref.shape[0]
    w_q, w_o, w_1, w_2 = (w.at[slot] for w in w_bufs)

    def saves(at, h_slot):
        sources = [h_scr.at[h_slot], a_scr, qkv_scr, o_scr, lse_t, h1_scr, a2_scr]
        return [pltpu.make_async_copy(src, out.at[at], out_sems.at[k]) for k, (src, out) in enumerate(zip(sources, outs))]

    def load(at, to):
        for k in range(FOUR):
            start_load(flags_ref, at, weights[k], w_bufs[k].at[to], w_sems.at[to, k])

    @pl.when(layer == 0)
    def _():
        load(0, 0)
        first = pltpu.make_async_copy(x_ref, h_scr.at[0], x_sem)
        first.start()
        first.wait()

    @pl.when(layer + 1 < n_layers)
    def _():
        load(layer + 1, 1 - slot)

    def finish(index):
        @pl.when(layer > 0)
        def _():
            saves(layer - 1, slot)[index].wait()

    wait_load(weights[0], w_q, w_sems.at[slot, 0])
    finish(1)
    finish(2)

    @pl.loop(0, seq // ROWS)
    def _(block):
        rows = rows_of(block)
        a = ln_apply(h_scr[slot, rows, :], stat_row(s_ref, ROW_G1), stat_row(s_ref, ROW_S1))
        a_scr[rows, :] = a
        for t in range(3):
            qkv_scr[rows, chunk(t)] = (mm(a, w_q[chunk(t), :], NT) + stat_row(s_ref, t)).astype(BF16)

    now = saves(layer, 1 - slot)
    now[1].start()
    now[2].start()
    finish(3)
    finish(4)
    lse_scr[...] = jnp.zeros_like(lse_scr)

    @pl.loop(0, PAIRS)
    def _(pair):
        attend(qkv_scr, o_scr, lse_scr, pair, seq)

    lse_t[...] = lse_scr[...].T[:N_STAT, :]
    now[3].start()
    now[4].start()
    for k in range(1, FOUR):
        wait_load(weights[k], (w_q, w_o, w_1, w_2)[k], w_sems.at[slot, k])
    finish(5)
    finish(6)
    finish(0)

    @pl.loop(0, seq // ROWS)
    def _(block):
        rows = rows_of(block)
        h1 = (h_scr[slot, rows, :].astype(F32) + mm(o_scr[rows, :], w_o[...], NN) + stat_row(s_ref, ROW_BO)).astype(BF16)
        h1_scr[rows, :] = h1
        a2 = ln_apply(h1, stat_row(s_ref, ROW_G2), stat_row(s_ref, ROW_S2))
        a2_scr[rows, :] = a2
        acc = stat_row(s_ref, ROW_B2)
        for j in range(w_1.shape[1] // WIDTH):
            pre = mm(a2, w_1[:, chunk(j)], NN) + stat_row(s_ref, ROW_FC + j)
            _, _, half = gelu_terms(pre)
            u = (pre * half).astype(BF16)
            if keep_u:
                u_scr[rows, chunk(j)] = u
            acc = acc + mm(u, w_2[chunk(j), :], NN)
        h_scr[1 - slot, rows, :] = (h1.astype(F32) + acc).astype(BF16)

    now[5].start()
    now[6].start()
    now[0].start()

    @pl.when(layer == n_layers - 1)
    def _():
        if keep_u:
            extra = pltpu.make_async_copy(u_scr, outs[-1], x_sem)
            extra.start()
            extra.wait()
        for copy in now:
            copy.wait()


def forward_stack(x, flags, small, weights, keep_u):
    seq = x.shape[0]
    n_layers = small.shape[0]
    n_fc = weights[2][0].shape[-1]
    stack = lambda cols: jax.ShapeDtypeStruct((n_layers, seq, cols), BF16)
    out_shape = [stack(WIDTH), stack(WIDTH), stack(3 * WIDTH), stack(WIDTH), jax.ShapeDtypeStruct((n_layers, N_STAT, seq), F32), stack(WIDTH), stack(WIDTH)]
    act = lambda cols: pltpu.VMEM((seq, cols), BF16)
    scratch = [pltpu.VMEM((2,) + own.shape[1:], BF16) for own, _ in weights]
    scratch += [pltpu.VMEM((2, seq, WIDTH), BF16), act(WIDTH), act(3 * WIDTH), act(WIDTH), pltpu.VMEM((seq, LANES), F32), pltpu.VMEM((N_STAT, seq), F32), act(WIDTH), act(WIDTH)]
    scratch += [pltpu.SemaphoreType.DMA((2, FOUR)), pltpu.SemaphoreType.DMA((7,)), pltpu.SemaphoreType.DMA]
    if keep_u:
        out_shape.append(jax.ShapeDtypeStruct((seq, n_fc), BF16))
        scratch.append(act(n_fc))
    flat = [w for pair in weights for w in pair]
    return pl.pallas_call(
        functools.partial(forward_body, keep_u),
        grid_spec=pltpu.PrefetchScalarGridSpec(
            num_scalar_prefetch=1,
            grid=(n_layers,),
            in_specs=[ANY, pl.BlockSpec((1,) + small.shape[1:], lambda l, f: (l, 0, 0))] + [ANY] * len(flat),
            out_specs=[ANY] * len(out_shape),
            scratch_shapes=scratch,
        ),
        out_shape=out_shape,
        compiler_params=pltpu.CompilerParams(vmem_limit_bytes=VMEM_LIMIT),
        cost_estimate=pl.CostEstimate(flops=n_layers * seq * WIDTH * (HEADS * WIDTH + FOUR * n_fc), bytes_accessed=n_layers * seq * WIDTH * HEADS, transcendentals=0),
        name="forward_stack",
    )(flags, x, small, *flat)


def picked_spec(block, index_map, picked):
    _, at = picked
    if at is None:
        return pl.BlockSpec(block, index_map)
    return pl.BlockSpec((None,) + block, lambda *ids: (at,) + index_map(*ids))


def attn_bwd_body(q_ref, k_ref, v_ref, do_ref, o_ref, lse_ref, dqkv_hbm, db_ref, dq_scr, delta_scr, stage, sems):
    pair = pl.program_id(0)
    last = pl.num_programs(0) - 1
    slot = pair % 2
    seq = q_ref.shape[0]
    n_blk = seq // BLK
    lane = iota((seq, LANES), 1)
    first = lane < HEAD

    def copies(at_pair, at_slot):
        return [pltpu.make_async_copy(stage.at[at_slot, t], dqkv_hbm.at[:, lanes_of(t * PAIRS + at_pair)], sems.at[at_slot, t]) for t in range(3)]

    @pl.when(pair >= 2)
    def _():
        for copy in copies(pair - 2, slot):
            copy.wait()

    causal_t = iota((BLK, BLK), 0) <= iota((BLK, BLK), 1)
    prod = do_ref[...].astype(F32) * o_ref[...].astype(F32)
    halves = lambda x: (jnp.where(first, x, jnp.zeros_like(x)), jnp.where(first, jnp.zeros_like(x), x))
    delta_scr[...] = jnp.where(lane == 0, *(row_sum(p) for p in halves(prod))).T[: delta_scr.shape[0], :]
    q_h, do_h, k_h = (halves(ref[...]) for ref in (q_ref, do_ref, k_ref))
    dq_scr[...] = jnp.zeros_like(dq_scr)
    sum_k = sum_v = jnp.zeros((1, LANES), F32)
    for j in range(n_blk):
        keys, rest = slice(j * BLK, (j + 1) * BLK), slice((j + 1) * BLK, seq)
        k_blk, v_blk = k_ref[keys, :], v_ref[keys, :]
        dk = dv = jnp.zeros((BLK, LANES), F32)
        for h in range(2):
            for rows in (keys, rest)[: 1 + (j + 1 < n_blk)]:
                q_p, do_p = q_h[h][rows], do_h[h][rows]
                lse = lse_ref[pl.ds(2 * pair + h, 1), rows]
                p_t = jnp.exp2(mm(k_blk, q_p, NT) * EXP_SCALE - lse)
                if rows is keys:
                    p_t = jnp.where(causal_t, p_t, 0.0)
                ds_t = (p_t * (mm(v_blk, do_p, NT) - delta_scr[h : h + 1, rows])).astype(BF16)
                dv = dv + mm(p_t.astype(BF16), do_p, NN)
                dk = dk + mm(ds_t, q_p, NN)
                dq_scr[rows, :] += mm(ds_t, k_h[h][keys], TN)
        dk, dv = (dk * SCALE).astype(BF16), dv.astype(BF16)
        stage[slot, 1, keys, :] = dk
        stage[slot, 2, keys, :] = dv
        sum_k, sum_v = sum_k + col_sum(dk.astype(F32)), sum_v + col_sum(dv.astype(F32))
    dq = (dq_scr[...] * SCALE).astype(BF16)
    stage[slot, 0] = dq
    for t, total in enumerate((col_sum(dq.astype(F32)), sum_k, sum_v)):
        db_ref[t] = jnp.broadcast_to(total, db_ref.shape[1:])
    for copy in copies(pair, slot):
        copy.start()

    @pl.when(pair == last)
    def _():
        for copy in copies(pair - 1, 1 - slot) + copies(pair, slot):
            copy.wait()


def attn_bwd(qkv, d_out, out, lse):
    seq = d_out.shape[0]
    block = (seq, LANES)
    column = lambda t: (lambda p: (0, t * PAIRS + p))
    return pl.pallas_call(
        attn_bwd_body,
        grid=(PAIRS,),
        in_specs=[picked_spec(block, column(t), qkv) for t in range(3)]
        + [pl.BlockSpec(block, column(0)), picked_spec(block, column(0), out), picked_spec((N_STAT, seq), lambda p: (0, 0), lse)],
        out_specs=[ANY, pl.BlockSpec((3, N_STAT, LANES), lambda p: (0, 0, p))],
        out_shape=[jax.ShapeDtypeStruct((seq, 3 * WIDTH), BF16), jax.ShapeDtypeStruct((3, N_STAT, WIDTH), F32)],
        scratch_shapes=[pltpu.VMEM(block, F32), pltpu.VMEM((N_STAT, seq), F32), pltpu.VMEM((2, 3) + block, BF16), pltpu.SemaphoreType.DMA((2, 3))],
        compiler_params=pltpu.CompilerParams(vmem_limit_bytes=VMEM_LIMIT),
        cost_estimate=pl.CostEstimate(flops=FOUR * FOUR * seq * seq * WIDTH, bytes_accessed=N_STAT * seq * WIDTH, transcendentals=0),
        name="attn_bwd",
    )(qkv[0], qkv[0], qkv[0], d_out, out[0], lse[0])


def row_call(body, layer, flags, rows_in, small, weights, out_cols, flops):
    tokens = rows_in[0][0].shape[-2]
    index_map = lambda i, f: (i, 0)
    in_specs = [picked_spec((ROWS, r[0].shape[-1]), index_map, r) for r in rows_in]
    in_specs.append(pl.BlockSpec((1,) + small.shape[1:], lambda i, f: (layer, 0, 0)))
    flat = [w for pair in weights for w in pair]
    return pl.pallas_call(
        functools.partial(body, layer),
        grid_spec=pltpu.PrefetchScalarGridSpec(
            num_scalar_prefetch=1,
            grid=(tokens // ROWS,),
            in_specs=in_specs + [ANY] * len(flat),
            out_specs=[pl.BlockSpec((ROWS, c), index_map) for c in out_cols] + [pl.BlockSpec((N_STAT, WIDTH), lambda i, f: (0, 0))],
            scratch_shapes=[pltpu.VMEM(own.shape[1:], BF16) for own, _ in weights] + [pltpu.SemaphoreType.DMA((len(weights),))],
        ),
        out_shape=[jax.ShapeDtypeStruct((tokens, c), BF16) for c in out_cols] + [jax.ShapeDtypeStruct((N_STAT, WIDTH), F32)],
        compiler_params=pltpu.CompilerParams(vmem_limit_bytes=VMEM_LIMIT),
        cost_estimate=pl.CostEstimate(flops=flops, bytes_accessed=tokens * sum(out_cols) * FOUR, transcendentals=0),
    )(flags, *(r for r, _ in rows_in), small, *flat)


def load_all(layer, flags_ref, sums_ref, pairs, bufs, sem):
    @pl.when(pl.program_id(0) == 0)
    def _():
        sums_ref[...] = jnp.zeros_like(sums_ref)
        for k, (pair, buf) in enumerate(zip(pairs, bufs)):
            start_load(flags_ref, layer, pair, buf, sem.at[k])
        for k, (pair, buf) in enumerate(zip(pairs, bufs)):
            wait_load(pair, buf, sem.at[k])


def mlp_bwd_body(save_u, layer, flags_ref, dh2_ref, a2_ref, h1_ref, s_ref, *refs):
    pairs = [refs[2 * k : 2 * k + 2] for k in range(3)]
    dpre_ref, dh1_ref, do_ref = refs[6:9]
    sums_ref, w_o, w_1, w_2, sem = refs[-5:]
    load_all(layer, flags_ref, sums_ref, pairs, (w_o, w_1, w_2), sem)

    def add_sum(row, value):
        sums_ref[row : row + 1, :] += value

    dh2 = dh2_ref[...]
    a2 = a2_ref[...]
    da2 = None
    for j in range(w_1.shape[1] // WIDTH):
        du = mm(dh2, w_2[chunk(j), :], NT).astype(BF16).astype(F32)
        pre = mm(a2, w_1[:, chunk(j)], NN) + stat_row(s_ref, ROW_FC + j)
        square, t, half = gelu_terms(pre)
        if save_u:
            refs[9][:, chunk(j)] = (pre * half).astype(BF16)
        slope = half + (0.5 * pre) * (1.0 - t * t) * (GELU_C + (3.0 * GELU_CA) * square)
        d_pre = du * slope
        add_sum(ROW_FC + j, col_sum(d_pre))
        d_pre = d_pre.astype(BF16)
        dpre_ref[:, chunk(j)] = d_pre
        part = mm(d_pre, w_1[:, chunk(j)], NT)
        da2 = part if da2 is None else da2 + part
    d_rows, d_gain, d_shift = ln_grad(h1_ref[...], stat_row(s_ref, ROW_G2), da2.astype(BF16).astype(F32))
    dh2_f = dh2.astype(F32)
    dh1 = (d_rows.astype(F32) + dh2_f).astype(BF16)
    dh1_ref[...] = dh1
    add_sum(ROW_BO, col_sum(dh1.astype(F32)))
    add_sum(ROW_G2, d_gain)
    add_sum(ROW_S2, d_shift)
    add_sum(ROW_B2, col_sum(dh2_f))
    do_ref[...] = mm(dh1, w_o[...], NT).astype(BF16)


def qkv_bwd_body(layer, flags_ref, dqkv_ref, h_ref, dh1_ref, s_ref, own_ref, peer_ref, dh_ref, sums_ref, w_q, sem):
    load_all(layer, flags_ref, sums_ref, [(own_ref, peer_ref)], [w_q], sem)
    da = mm(dqkv_ref[...], w_q[...], NN).astype(BF16).astype(F32)
    d_rows, d_gain, d_shift = ln_grad(h_ref[...], stat_row(s_ref, ROW_G1), da)
    dh_ref[...] = (d_rows.astype(F32) + dh1_ref[...].astype(F32)).astype(BF16)
    sums_ref[ROW_G1 : ROW_G1 + 1, :] += d_gain
    sums_ref[ROW_S1 : ROW_S1 + 1, :] += d_shift


def wgrad_body(plan, *refs):
    n_pair = len(plan)
    lhs_refs = refs[0 : 2 * n_pair : 2]
    rhs_refs = refs[1 : 2 * n_pair : 2]
    out_ref, send_buf, recv_buf, send_sems, recv_sems = refs[2 * n_pair :]
    pos = lax.axis_index("pp")
    core = pos % 2
    partner = {"pp": pos + 1 - 2 * core}
    barrier = pltpu.get_barrier_semaphore()
    pl.semaphore_signal(barrier, device_id=partner, device_id_type=MESH_ID)
    pl.semaphore_wait(barrier)

    def copy(tile):
        return pltpu.make_async_remote_copy(send_buf.at[tile], recv_buf.at[tile], send_sems.at[tile], recv_sems.at[tile], device_id=partner, device_id_type=MESH_ID)

    def product(index, tile, half):
        unit, col = (tile, 0) if plan[index][1] == 1 else (0, tile)
        lhs = lhs_refs[index][:, pl.ds(pl.multiple_of(unit * WIDTH + half * HALF, LANES), HALF)]
        rhs = rhs_refs[index][:, pl.ds(pl.multiple_of(col * WIDTH, LANES), WIDTH)]
        return mm(lhs, rhs, TN)

    counts = [units * cols for units, cols in plan]
    starts = [sum(counts[:index]) for index in range(n_pair)]
    total = sum(counts)
    for index in range(n_pair):

        @pl.loop(0, counts[index])
        def _(tile, index=index, base=starts[index]):
            send_buf[base + tile] = product(index, tile, 1 - core)

            @pl.when(base + tile > 0)
            def _():
                copy(base + tile - 1).start()

    for index in range(n_pair):

        @pl.loop(0, counts[index])
        def _(tile, index=index, base=starts[index]):
            mine = product(index, tile, core)

            @pl.when(base + tile == 0)
            def _():
                copy(total - 1).start()

            copy(base + tile).wait_recv()
            out_ref[base + tile] = (mine + recv_buf[base + tile]).astype(BF16)

    @pl.loop(0, total)
    def _(tile):
        copy(tile).wait_send()


def wgrad(pairs, collective_id):
    flat = [side for pair in pairs for side in pair]
    plan = tuple((lhs[0].shape[-1] // WIDTH, rhs[0].shape[-1] // WIDTH) for lhs, rhs in pairs)
    total = sum(u * c for u, c in plan)
    seq = flat[0][0].shape[-2]
    return pl.pallas_call(
        functools.partial(wgrad_body, plan),
        grid=(1,),
        in_specs=[picked_spec((seq, side[0].shape[-1]), lambda i: (0, 0), side) for side in flat],
        out_specs=pl.BlockSpec((total, HALF, WIDTH), lambda i: (0, 0, 0)),
        out_shape=jax.ShapeDtypeStruct((total, HALF, WIDTH), BF16),
        scratch_shapes=[pltpu.VMEM((total, HALF, WIDTH), F32)] * 2 + [pltpu.SemaphoreType.DMA((total,))] * 2,
        compiler_params=pltpu.CompilerParams(collective_id=collective_id, has_side_effects=True, vmem_limit_bytes=VMEM_LIMIT),
        cost_estimate=pl.CostEstimate(flops=2 * total * seq * WIDTH * WIDTH, bytes_accessed=total * FOUR * WIDTH * WIDTH, transcendentals=0),
    )(*(side[0] for side in flat))


def layer_backward(dh2, saved, w, layer, exchange):
    h, a, qkv, o, lse, h1, a2, u = saved
    flags, small, w_qkv, w_attn, w_fc, w_proj = w
    tokens, n_fc = dh2.shape[0], w_fc[0].shape[-1]
    split = u is not None
    own, received = [], []

    def send(pairs, collective_id, follow):
        g = wgrad(pairs, collective_id)
        follow, g = lax.optimization_barrier((follow, g))
        received.append(exchange(g))
        own.append(g)
        return follow

    whole = lambda x: (x, None)
    if split:
        dh2 = send([(whole(u), whole(dh2))], 1, dh2)
    outs = row_call(
        functools.partial(mlp_bwd_body, not split), layer, flags, [whole(dh2), a2, h1], small, [w_attn, w_fc, w_proj],
        [n_fc, WIDTH, WIDTH] + [n_fc] * (not split), 2 * tokens * WIDTH * (WIDTH + 3 * n_fc),
    )
    d_pre, dh1, do, sums = outs[0], outs[1], outs[2], outs[-1]
    pair_fc = (a2, whole(d_pre))
    if split:
        do = send([pair_fc], 2, do)
    else:
        do = send([(whole(outs[3]), whole(dh2)), pair_fc], 3, do)
    dqkv, d_bqkv = attn_bwd(qkv, do, o, lse)
    dqkv = send([(whole(dqkv), a), (o, whole(dh1))], FOUR, dqkv)
    dh, sums_q = row_call(qkv_bwd_body, layer, flags, [whole(dqkv), h, whole(dh1)], small, [w_qkv], [WIDTH], 6 * tokens * WIDTH * WIDTH)
    small_grads = jnp.concatenate([d_bqkv[:, 0], sums[ROW_FC:ROW_G1], sums_q[ROW_G1:ROW_BO], sums[ROW_BO : ROW_B2 + 1]], axis=0)
    return dh, own, received, small_grads


def total_of(parts):
    a, b, c, d = (p[0].astype(F32) for p in parts)
    return (a + b) + (c + d)


def part_specs(parts, blk, index_of):
    return [pl.BlockSpec(blk, functools.partial(index_of, off)) for _, off in parts]


def send_total_body(flags_ref, *refs):
    out_ref = refs[-1]
    for flag in range(2):

        @pl.when(flags_ref[0] == flag)
        def _(flag=flag):
            out_ref[0] = total_of(refs[FOUR * flag : FOUR * (flag + 1)])


def send_total(flags, outer, inner):
    blk = (1, HALF, WIDTH)
    return pl.pallas_call(
        send_total_body,
        grid_spec=pltpu.PrefetchScalarGridSpec(
            num_scalar_prefetch=1,
            grid=(FOUR,),
            in_specs=part_specs(outer, blk, lambda off, i, f: (off + i * (1 - f[0]), 0, 0)) + part_specs(inner, blk, lambda off, i, f: (off + i * f[0], 0, 0)),
            out_specs=pl.BlockSpec(blk, lambda i, f: (i, 0, 0)),
        ),
        out_shape=jax.ShapeDtypeStruct((FOUR, HALF, WIDTH), F32),
        cost_estimate=pl.CostEstimate(flops=HALF * WIDTH * BLK, bytes_accessed=HALF * WIDTH * FOUR * HEADS, transcendentals=0),
        name="send_total",
    )(flags, *(p for p, _ in outer + inner))


def final_total_body(flags_ref, *refs):
    recv_ref, out_ref = refs[2 * FOUR], refs[-1]
    mine = pl.program_id(1) == flags_ref[2]
    for flag in range(2):

        @pl.when(mine & (flags_ref[0] == 1 - flag))
        def _(flag=flag):
            out_ref[0] = total_of(refs[FOUR * flag : FOUR * (flag + 1)])

    @pl.when(jnp.logical_not(mine))
    def _():
        out_ref[0] = recv_ref[0]


def final_total(flags, outer, inner, recv, first, count, by_rows, prev):
    blk = (1, HALF, WIDTH)
    in_specs = part_specs(outer, blk, lambda off, i, h, f: (off + i * f[0], 0, 0)) + part_specs(inner, blk, lambda off, i, h, f: (off + i * (1 - f[0]), 0, 0))
    in_specs.append(pl.BlockSpec(blk, lambda i, h, f: (first + i, 0, 0)))
    args = [p for p, _ in outer + inner] + [recv]
    aliases = {}
    if prev is not None:
        in_specs.append(ANY)
        args.append(prev)
        aliases = {len(args): 0}
    long, wide = (count, 1) if by_rows else (1, count)
    out_map = (lambda i, h, f: (f[1], 2 * i + h, 0)) if by_rows else (lambda i, h, f: (f[1], h, i))
    return pl.pallas_call(
        final_total_body,
        grid_spec=pltpu.PrefetchScalarGridSpec(num_scalar_prefetch=1, grid=(count, 2), in_specs=in_specs, out_specs=pl.BlockSpec(blk, out_map)),
        out_shape=jax.ShapeDtypeStruct((2, long * WIDTH, wide * WIDTH), F32),
        input_output_aliases=aliases,
        cost_estimate=pl.CostEstimate(flops=count * HALF * WIDTH * BLK, bytes_accessed=count * WIDTH * WIDTH * HEADS, transcendentals=0),
        name="final_total",
    )(flags, *args)


def solution(mesh):
    n_layers = mesh.shape['pp']
    data_spec = P(('dp', 'pp'))
    weight_spec = P('pp')
    swap = [(i, i ^ 1) for i in range(n_layers)]
    cross = [(i, i ^ 2) for i in range(n_layers)]

    def per_device(x_loc, dy_loc, w_qkv, w_attn, w_fc, w_proj, b_qkv, b_fc, vec_d):
        pos = lax.axis_index('pp')
        core = pos % 2
        upper = pos // 2
        outer_dev = 1 - (core ^ upper)
        width, n_fc = WIDTH, w_fc.shape[-1]
        own = (
            jnp.transpose(w_qkv, (0, 1, 2, 4, 5, 6, 3)).reshape(2, 3 * width, width),
            w_attn.reshape(2, width, width),
            w_fc.reshape(2, width, n_fc),
            w_proj.reshape(2, n_fc, width),
        )
        own_small = jnp.concatenate([b_qkv.reshape(2, -1), b_fc.reshape(2, -1), vec_d.reshape(2, -1)], axis=1)
        trade = lambda t: lax.ppermute(t, 'pp', swap)
        pick = lambda t, at: lax.dynamic_index_in_dim(t, at, 0, False)

        def by_sequence(mine):
            got = trade(pick(mine, 1 - core))
            return jnp.where(core == 0, mine[0], got), jnp.where(core == 0, got, mine[1])

        def by_micro(first, second):
            got = trade(jnp.where(core == 0, second, first))
            return jnp.where(core == 0, jnp.stack([first, got]), jnp.stack([got, second]))

        xs = by_sequence(x_loc[0])
        peer_small = trade(own_small)
        peer = tuple(trade(t) for t in own)
        flags = jnp.stack([jnp.stack([outer_dev if l in (0, n_layers - 1) else 1 - outer_dev, upper if l < 2 else 1 - upper]) for l in range(n_layers)])
        small_of = lambda l: jnp.where(flags[l, 0] == 1, pick(own_small, flags[l, 1]), pick(peer_small, flags[l, 1]))
        small_w = jnp.stack([small_of(l) for l in range(n_layers)]).astype(F32).reshape(n_layers, -1, width)
        weights = tuple(zip(own, peer))
        ys, dxs, smalls = [], [], []
        parts = [[] for _ in range(n_layers)]
        dys = None
        for micro in range(2):
            x = xs[micro]
            if micro:
                x, _ = lax.optimization_barrier((x, dxs[0]))
            first = micro == 0
            res = forward_stack(x, flags, small_w, weights, first)
            if first:
                late, _ = lax.optimization_barrier((dy_loc, peer[2]))
                dys = by_sequence(late[0])
            ys.append(res[0][n_layers - 1])
            d = dys[micro]
            for layer in reversed(range(n_layers)):
                saved = [(res[0], layer - 1) if layer else (x, None)] + [(r, layer) for r in res[1:7]]
                saved.append(res[7] if first and layer == n_layers - 1 else None)
                d, sent, got, small = layer_backward(d, saved, (flags, small_w) + weights, layer, lambda g: lax.ppermute(g, 'pp', cross))
                smalls.append(small)
                parts[layer].append((sent, got))
            dxs.append(d)
        small = jnp.stack(smalls).reshape(2 * n_layers, -1)
        small = (small + trade(small)).astype(BF16)
        both = jnp.stack([small, lax.ppermute(small, 'pp', cross)]).astype(F32)
        both = both[:, :n_layers] + both[:, n_layers:]
        small = both[0] + both[1]
        small = jnp.stack([pick(small, n_layers - 1 - pos), pick(small, pos)])

        def pieces(layer, group):
            picked = []
            for which in range(2):
                for sets in parts[layer]:
                    arrays = sets[which]
                    if group == 2:
                        picked.append((arrays[-1], 0))
                    else:
                        picked.append((arrays[group], 0) if len(arrays) > 2 else (arrays[0], FOUR * group))
            return picked

        outs = [None] * FOUR
        plans = (((3, 0, FOUR, True),), ((2, 0, FOUR, False),), ((0, 0, 3, True), (1, 3, 1, True)))
        after = d
        for high in (True, False):
            outer_layer, inner_layer, copy = (3, 2, 1 - upper) if high else (0, 1, upper)
            for group, slots in enumerate(plans):
                order, _ = lax.optimization_barrier((jnp.stack([outer_dev, copy, core]), after))
                outer, inner = pieces(outer_layer, group), pieces(inner_layer, group)
                sent = send_total(order, outer, inner)
                recv = trade(sent)
                for slot, first, count, by_rows in slots:
                    shifted = [[(p, off + first) for p, off in side] for side in (outer, inner)]
                    outs[slot] = final_total(order, *shifted, recv, first, count, by_rows, outs[slot])
                after = sent if high else outs[slots[0][0]]
            if high:
                after, *outs = lax.optimization_barrier([after] + outs)
        n_qkv = 3 * width
        g_bqkv = small[:, :n_qkv].reshape((1,) + b_qkv.shape[1:])
        g_bfc = small[:, n_qkv : n_qkv + n_fc].reshape((1,) + b_fc.shape[1:])
        g_vec = small[:, n_qkv + n_fc :].reshape((1,) + vec_d.shape[1:])
        g_qkv = jnp.transpose(outs[0].reshape(1, 2, 1, 3, HEADS, HEAD, width), (0, 1, 2, 6, 3, 4, 5))
        g_attn, g_fc, g_proj = (out.reshape((1,) + t.shape[1:]) for out, t in zip(outs[1:], (w_attn, w_fc, w_proj)))
        y, dx = by_micro(*ys), by_micro(*dxs)
        return (y[None], dx[None], g_qkv, g_attn, g_fc, g_proj, g_bqkv, g_bfc, g_vec)

    return jax.shard_map(per_device, mesh=mesh, in_specs=(data_spec,) * 2 + (weight_spec,) * 7, out_specs=(data_spec,) * 9, check_vma=False)
```

time: 7210 us -> 2510 us (0.35)
  starting transfers between devices: 2120 us -> 28.4 us
  matrix products: 2020 us -> 0 us
  Pallas kernels: 0 us -> 1450 us
  local copies, waits for them, and re-layouts: 800 us -> 23.9 us
  waiting for transfers between devices: 1590 us -> 952 us
  other arithmetic: 573 us -> 27.3 us
    ppermute x34, starting transfers between devices: 2120 us -> 28.4 us  [the longest x17 23.1 us: per_device(): lax.ppermute(g, 'pp', cross)]
    dot_general x80 -> x0, matrix products: 1660 us -> none  [the longest x16 497 us: gpt_layer(): jnp.einsum('bhqk,bkhe->bqhe', attn_probs, value_heads, preferred_element_...]
    pallas_call x0 -> x57, Pallas kernels: none -> 1450 us  [the longest x16 357 us: row_call(): pl.pallas_call(functools.partial(body, layer), grid_spec=pltpu.PrefetchSc...]
    ppermute x34, waiting for transfers between devices: 1530 us -> 952 us  [the longest x17 915 us: per_device(): lax.ppermute(g, 'pp', cross)]
    sub x8 -> x0, matrix products: 367 us -> none  [gpt_layer(): attn_probs = jax.nn.softmax(scores, axis=-1).astype(jnp.bfloat16)]
    convert_element_type x32 -> x3, other arithmetic: 232 us -> 0.8 us  [the longest x1 0.7 us: per_device(): jnp.stack([small_of(l) for l in range(n_layers)]).astype(F32)]
    convert_element_type x56 -> x0, local copies, waits for them, and re-layouts: 185 us -> none  [the longest x8 101 us: gpt_layer(): (qkv_proj + b_qkv.reshape(3 * d_model).astype(jnp.float32)).astype(jnp.bf...]
    reshape x12 -> x4, local copies, waits for them, and re-layouts: 144 us -> 2.12 us  [the longest x1 0.72 us: per_device(): g_bqkv = small[:, :n_qkv].reshape((1,) + b_qkv.shape[1:])]
  transfers between devices with their start and end apart: 38 -> 34, of which waited for: 11 -> 11; matrix products, arithmetic and copies ran while one was open for 47% -> 2% of each run, Pallas kernels for 0% -> 22%
where the time goes in v1:
time: 2510 us; the launch traced here: 2500 us
  Pallas kernels  1450 us (58%)
  waiting for transfers between devices  952 us (38%)
  starting transfers between devices  28.4 us (1%)
  other arithmetic  27.3 us (1%)
    ppermute x17, waiting for transfers between devices, per_device(): lax.ppermute(g, 'pp', cross)  915 us
    pallas_call x16, Pallas kernels, row_call(): pl.pallas_call(functools.partial(body, layer), grid_spec=pltpu.PrefetchSc...  357 us
    pallas_call x2, Pallas kernels, forward_stack(): pl.pallas_call(functools.partial(forward_body, keep_u), grid_spec=pltpu.P...  355 us
    pallas_call x17, Pallas kernels, wgrad(): pl.pallas_call(functools.partial(wgrad_body, plan), grid=(1,), in_specs=[...  331 us
    pallas_call x8, Pallas kernels, attn_bwd(): pl.pallas_call(attn_bwd_body, grid=(PAIRS,), in_specs=[picked_spec(block,...  273 us
    pallas_call x8, Pallas kernels, final_total(): pl.pallas_call(final_total_body, grid_spec=pltpu.PrefetchScalarGridSpec(n...  91 us
  transfers between devices with their start and end apart: 34, of which 11 were waited for; matrix products, arithmetic and copies ran while one was open for 2% of the time, Pallas kernels for 22%

profile of v1, /device:TPU:0, one launch (start us, length us, event | category | flops | bytes accessed | tf_op | source)
XLA Modules:
  0.0 2497.2 jit_solution(2200964036369425494)
XLA Ops:
  6.8 36.3 %collective-permute-done.1 = bf16[2,9984]{1,0:T(2,128)(2,1)S(1)} collective-permute-done((bf16[2,9984]{1,0:T(2,128)(2,1)S(1)}, bf16[2,9984]{1,0:T(2,128)(2,1)S(1)}, u32[]{:S(2)}, u32[]{:S(2)}) %collective-permute-start.1) | collective-permute-done | bytes 39968 | tf_op jit(solution)/shard_map/ppermute | solution.py:631
  63.1 178.6 %forward_stack.2 = (bf16[4,1024,768]{2,1,0:T(8,128)(2,1)}, bf16[4,1024,768]{2,1,0:T(8,128)(2,1)}, bf16[4,1024,2304]{2,1,0:T(8,128)(2,1)}, bf16[4,1024,768]{2,1,0...) custom-call(s32[4,2]{1,0:T(4,128)} %pad_add_fusion.flags_ref, ...), custom_call_target="tpu_custom_call" | custom-call | flops 67645734912 | bytes 37748736 | tf_op jit(solution)/shard_map/forward_stack/pallas_call | solution.py:265
  245.1 15.4 shard_map.160.refs_0_
  260.6 31.0 %shard_map.161 = (bf16[1024,3072]{1,0:T(8,128)(2,1)}, bf16[1024,768]{1,0:T(8,128)(2,1)}, bf16[1024,768]{1,0:T(8,128)(2,1)}, f32[16,768]{1,0:T(8,128)}) custom-call(s32[4,2]{1,0:T(4,128)} %pad_add_fusion.flags_ref, bf16[1024,768]{1,0:T(8,128)(2,1)} %get-tuple-element.144.refs_1_.dh2_ref, bf16[4,1024,768]{2,1,0:T(8,128)(2,1)} %get-tuple-element.145.a2_ref.refs_0_.refs_2_, ...), custom_call_target="tpu_custom_call" | custom-call | flops 15703474176 | bytes 18874368 | tf_op jit(solution)/shard_map/pallas_call | solution.py:368
  291.6 15.3 shard_map.162.refs_0_
  306.9 34.1 %attn_bwd.8 = (bf16[1024,2304]{1,0:T(8,128)(2,1)}, f32[3,16,768]{2,1,0:T(8,128)}) custom-call(bf16[4,1024,2304]{2,1,0:T(8,128)(2,1)} %get-tuple-element.141.q_ref.k_ref.v_ref, bf16[4,1024,2304]{2,1,0:T(8,128)(2,1)} %get-tuple-element.141.q_ref.k_ref.v_ref, bf16[4,1024,2304]{2,1,0:T(8,128)(2,1)} %get-tuple-element.141.q_ref.k_ref.v_ref, ...), custom_call_target="tpu_custom_call" | custom-call | flops 12884901888 | bytes 12582912 | tf_op jit(solution)/shard_map/attn_bwd/pallas_call | solution.py:348
  341.0 15.5 shard_map.163.refs_0_
  368.4 32.8 %shard_map.165 = (bf16[1024,3072]{1,0:T(8,128)(2,1)}, bf16[1024,768]{1,0:T(8,128)(2,1)}, bf16[1024,768]{1,0:T(8,128)(2,1)}, bf16[1024,3072]{1,0:T(8,128)(2,1)}, f32[16,768]{1,0:T(8,128)}) custom-call(s32[4,2]{1,0:T(4,128)} %pad_add_fusion.flags_ref, bf16[1024,768]{1,0:T(8,128)(2,1)} %get-tuple-element.156.dh2_ref.refs_1_, ...), custom_call_target="tpu_custom_call" | custom-call | flops 15703474176 | bytes 31457280 | tf_op jit(solution)/shard_map/pallas_call | solution.py:368
  401.2 25.0 %shard_map.166.refs_4_ = bf16[8,384,768]{2,1,0:T(8,128)(2,1)} custom-call(bf16[1024,3072]{1,0:T(8,128)(2,1)} %get-tuple-element.158.refs_0_, bf16[1024,768]{1,0:T(8,128)(2,1)} %get-tuple-element.156.dh2_ref.refs_1_, bf16[4,1024,768]{2,1,0:T(8,128)(2,1)} %get-tuple-element.145.a2_ref.refs_0_.refs_2_, bf16[1024,3072]{1,0:T(8,128)(2,1)} %get-tuple-element.159.refs_3_), custom_call_target="tpu_custom_call" | custom-call | flops 9663676416 | bytes 18874368 | tf_op jit(solution)/shard_map/pallas_call | solution.py:495
  426.2 34.1 %attn_bwd.9 = (bf16[1024,2304]{1,0:T(8,128)(2,1)}, f32[3,16,768]{2,1,0:T(8,128)}) custom-call(bf16[4,1024,2304]{2,1,0:T(8,128)(2,1)} %get-tuple-element.141.q_ref.k_ref.v_ref, bf16[4,1024,2304]{2,1,0:T(8,128)(2,1)} %get-tuple-element.141.q_ref.k_ref.v_ref, bf16[4,1024,2304]{2,1,0:T(8,128)(2,1)} %get-tuple-element.141.q_ref.k_ref.v_ref, ...), custom_call_target="tpu_custom_call" | custom-call | flops 12884901888 | bytes 12582912 | tf_op jit(solution)/shard_map/attn_bwd/pallas_call | solution.py:348
  460.3 15.6 shard_map.167.refs_4_
  487.7 32.8 %shard_map.169 = (bf16[1024,3072]{1,0:T(8,128)(2,1)}, bf16[1024,768]{1,0:T(8,128)(2,1)}, bf16[1024,768]{1,0:T(8,128)(2,1)}, bf16[1024,3072]{1,0:T(8,128)(2,1)}, f32[16,768]{1,0:T(8,128)}) custom-call(s32[4,2]{1,0:T(4,128)} %pad_add_fusion.flags_ref, bf16[1024,768]{1,0:T(8,128)(2,1)} %get-tuple-element.164.dh2_ref.refs_1_, ...), custom_call_target="tpu_custom_call" | custom-call | flops 15703474176 | bytes 31457280 | tf_op jit(solution)/shard_map/pallas_call | solution.py:368
  520.4 25.0 %shard_map.170.refs_4_ = bf16[8,384,768]{2,1,0:T(8,128)(2,1)} custom-call(bf16[1024,3072]{1,0:T(8,128)(2,1)} %get-tuple-element.166.refs_0_, bf16[1024,768]{1,0:T(8,128)(2,1)} %get-tuple-element.164.dh2_ref.refs_1_, bf16[4,1024,768]{2,1,0:T(8,128)(2,1)} %get-tuple-element.145.a2_ref.refs_0_.refs_2_, bf16[1024,3072]{1,0:T(8,128)(2,1)} %get-tuple-element.167.refs_3_), custom_call_target="tpu_custom_call" | custom-call | flops 9663676416 | bytes 18874368 | tf_op jit(solution)/shard_map/pallas_call | solution.py:495
  545.4 34.0 %attn_bwd.10 = (bf16[1024,2304]{1,0:T(8,128)(2,1)}, f32[3,16,768]{2,1,0:T(8,128)}) custom-call(bf16[4,1024,2304]{2,1,0:T(8,128)(2,1)} %get-tuple-element.141.q_ref.k_ref.v_ref, bf16[4,1024,2304]{2,1,0:T(8,128)(2,1)} %get-tuple-element.141.q_ref.k_ref.v_ref, bf16[4,1024,2304]{2,1,0:T(8,128)(2,1)} %get-tuple-element.141.q_ref.k_ref.v_ref, ...), custom_call_target="tpu_custom_call" | custom-call | flops 12884901888 | bytes 12582912 | tf_op jit(solution)/shard_map/attn_bwd/pallas_call | solution.py:348
  579.5 15.6 shard_map.171.refs_4_
  607.0 33.1 %shard_map.173 = (bf16[1024,3072]{1,0:T(8,128)(2,1)}, bf16[1024,768]{1,0:T(8,128)(2,1)}, bf16[1024,768]{1,0:T(8,128)(2,1)}, bf16[1024,3072]{1,0:T(8,128)(2,1)}, f32[16,768]{1,0:T(8,128)}) custom-call(s32[4,2]{1,0:T(4,128)} %pad_add_fusion.flags_ref, bf16[1024,768]{1,0:T(8,128)(2,1)} %get-tuple-element.172.dh2_ref.refs_1_, ...), custom_call_target="tpu_custom_call" | custom-call | flops 15703474176 | bytes 31457280 | tf_op jit(solution)/shard_map/pallas_call | solution.py:368
  640.1 25.0 shard_map.174.refs_0_
  665.0 34.1 %attn_bwd.11 = (bf16[1024,2304]{1,0:T(8,128)(2,1)}, f32[3,16,768]{2,1,0:T(8,128)}) custom-call(bf16[4,1024,2304]{2,1,0:T(8,128)(2,1)} %get-tuple-element.141.q_ref.k_ref.v_ref, bf16[4,1024,2304]{2,1,0:T(8,128)(2,1)} %get-tuple-element.141.q_ref.k_ref.v_ref, bf16[4,1024,2304]{2,1,0:T(8,128)(2,1)} %get-tuple-element.141.q_ref.k_ref.v_ref, ...), custom_call_target="tpu_custom_call" | custom-call | flops 12884901888 | bytes 12582912 | tf_op jit(solution)/shard_map/attn_bwd/pallas_call | solution.py:348
  699.2 15.6 shard_map.175.refs_0_
  726.7 176.6 %forward_stack.3 = (bf16[4,1024,768]{2,1,0:T(8,128)(2,1)}, bf16[4,1024,768]{2,1,0:T(8,128)(2,1)}, bf16[4,1024,2304]{2,1,0:T(8,128)(2,1)}, bf16[4,1024,768]{2,1,0...) custom-call(s32[4,2]{1,0:T(4,128)} %pad_add_fusion.flags_ref, ...), custom_call_target="tpu_custom_call" | custom-call | flops 67645734912 | bytes 37748736 | tf_op jit(solution)/shard_map/forward_stack/pallas_call | solution.py:265
  903.2 33.1 %shard_map.177 = (bf16[1024,3072]{1,0:T(8,128)(2,1)}, bf16[1024,768]{1,0:T(8,128)(2,1)}, bf16[1024,768]{1,0:T(8,128)(2,1)}, bf16[1024,3072]{1,0:T(8,128)(2,1)}, f32[16,768]{1,0:T(8,128)}) custom-call(s32[4,2]{1,0:T(4,128)} %pad_add_fusion.flags_ref, bf16[1024,768]{1,0:T(8,128)(2,1)} %get-tuple-element.296.dh2_ref.refs_1_, ...), custom_call_target="tpu_custom_call" | custom-call | flops 15703474176 | bytes 31457280 | tf_op jit(solution)/shard_map/pallas_call | solution.py:368
  936.3 25.0 %shard_map.178.refs_1_ = bf16[8,384,768]{2,1,0:T(8,128)(2,1)} custom-call(bf16[1024,3072]{1,0:T(8,128)(2,1)} %get-tuple-element.187.refs_0_, bf16[1024,768]{1,0:T(8,128)(2,1)} %get-tuple-element.296.dh2_ref.refs_1_, bf16[4,1024,768]{2,1,0:T(8,128)(2,1)} %get-tuple-element.184.a2_ref.refs_2_, bf16[1024,3072]{1,0:T(8,128)(2,1)} %get-tuple-element.188.refs_3_), custom_call_target="tpu_custom_call" | custom-call | flops 9663676416 | bytes 18874368 | tf_op jit(solution)/shard_map/pallas_call | solution.py:495
  961.3 34.1 %attn_bwd.12 = (bf16[1024,2304]{1,0:T(8,128)(2,1)}, f32[3,16,768]{2,1,0:T(8,128)}) custom-call(bf16[4,1024,2304]{2,1,0:T(8,128)(2,1)} %get-tuple-element.183.q_ref.k_ref.v_ref, bf16[4,1024,2304]{2,1,0:T(8,128)(2,1)} %get-tuple-element.183.q_ref.k_ref.v_ref, bf16[4,1024,2304]{2,1,0:T(8,128)(2,1)} %get-tuple-element.183.q_ref.k_ref.v_ref, ...), custom_call_target="tpu_custom_call" | custom-call | flops 12884901888 | bytes 12582912 | tf_op jit(solution)/shard_map/attn_bwd/pallas_call | solution.py:348
  995.4 15.6 shard_map.179.refs_1_
  1022.9 33.0 %shard_map.181 = (bf16[1024,3072]{1,0:T(8,128)(2,1)}, bf16[1024,768]{1,0:T(8,128)(2,1)}, bf16[1024,768]{1,0:T(8,128)(2,1)}, bf16[1024,3072]{1,0:T(8,128)(2,1)}, f32[16,768]{1,0:T(8,128)}) custom-call(s32[4,2]{1,0:T(4,128)} %pad_add_fusion.flags_ref, bf16[1024,768]{1,0:T(8,128)(2,1)} %get-tuple-element.196.dh2_ref.refs_1_, ...), custom_call_target="tpu_custom_call" | custom-call | flops 15703474176 | bytes 31457280 | tf_op jit(solution)/shard_map/pallas_call | solution.py:368
  1055.9 25.0 %shard_map.182.refs_5_ = bf16[8,384,768]{2,1,0:T(8,128)(2,1)} custom-call(bf16[1024,3072]{1,0:T(8,128)(2,1)} %get-tuple-element.198.refs_0_, bf16[1024,768]{1,0:T(8,128)(2,1)} %get-tuple-element.196.dh2_ref.refs_1_, bf16[4,1024,768]{2,1,0:T(8,128)(2,1)} %get-tuple-element.184.a2_ref.refs_2_, bf16[1024,3072]{1,0:T(8,128)(2,1)} %get-tuple-element.199.refs_3_), custom_call_target="tpu_custom_call" | custom-call | flops 9663676416 | bytes 18874368 | tf_op jit(solution)/shard_map/pallas_call | solution.py:495
  1081.0 34.0 %attn_bwd.13 = (bf16[1024,2304]{1,0:T(8,128)(2,1)}, f32[3,16,768]{2,1,0:T(8,128)}) custom-call(bf16[4,1024,2304]{2,1,0:T(8,128)(2,1)} %get-tuple-element.183.q_ref.k_ref.v_ref, bf16[4,1024,2304]{2,1,0:T(8,128)(2,1)} %get-tuple-element.183.q_ref.k_ref.v_ref, bf16[4,1024,2304]{2,1,0:T(8,128)(2,1)} %get-tuple-element.183.q_ref.k_ref.v_ref, ...), custom_call_target="tpu_custom_call" | custom-call | flops 12884901888 | bytes 12582912 | tf_op jit(solution)/shard_map/attn_bwd/pallas_call | solution.py:348
  1115.0 15.6 shard_map.183.refs_5_
  1149.4 32.8 %shard_map.185 = (bf16[1024,3072]{1,0:T(8,128)(2,1)}, bf16[1024,768]{1,0:T(8,128)(2,1)}, bf16[1024,768]{1,0:T(8,128)(2,1)}, bf16[1024,3072]{1,0:T(8,128)(2,1)}, f32[16,768]{1,0:T(8,128)}) custom-call(s32[4,2]{1,0:T(4,128)} %pad_add_fusion.flags_ref, bf16[1024,768]{1,0:T(8,128)(2,1)} %get-tuple-element.204.dh2_ref.refs_1_, ...), custom_call_target="tpu_custom_call" | custom-call | flops 15703474176 | bytes 31457280 | tf_op jit(solution)/shard_map/pallas_call | solution.py:368
  1182.2 25.0 %shard_map.186.refs_5_ = bf16[8,384,768]{2,1,0:T(8,128)(2,1)} custom-call(bf16[1024,3072]{1,0:T(8,128)(2,1)} %get-tuple-element.206.refs_0_, bf16[1024,768]{1,0:T(8,128)(2,1)} %get-tuple-element.204.dh2_ref.refs_1_, bf16[4,1024,768]{2,1,0:T(8,128)(2,1)} %get-tuple-element.184.a2_ref.refs_2_, bf16[1024,3072]{1,0:T(8,128)(2,1)} %get-tuple-element.207.refs_3_), custom_call_target="tpu_custom_call" | custom-call | flops 9663676416 | bytes 18874368 | tf_op jit(solution)/shard_map/pallas_call | solution.py:495
  1207.2 34.1 %attn_bwd.14 = (bf16[1024,2304]{1,0:T(8,128)(2,1)}, f32[3,16,768]{2,1,0:T(8,128)}) custom-call(bf16[4,1024,2304]{2,1,0:T(8,128)(2,1)} %get-tuple-element.183.q_ref.k_ref.v_ref, bf16[4,1024,2304]{2,1,0:T(8,128)(2,1)} %get-tuple-element.183.q_ref.k_ref.v_ref, bf16[4,1024,2304]{2,1,0:T(8,128)(2,1)} %get-tuple-element.183.q_ref.k_ref.v_ref, ...), custom_call_target="tpu_custom_call" | custom-call | flops 12884901888 | bytes 12582912 | tf_op jit(solution)/shard_map/attn_bwd/pallas_call | solution.py:348
  1241.3 15.6 shard_map.187.refs_5_
  1268.8 119.3 %collective-permute-done.14.refs_2_ = bf16[4,384,768]{2,1,0:T(8,128)(2,1)} collective-permute-done((bf16[4,384,768]{2,1,0:T(8,128)(2,1)}, bf16[4,384,768]{2,1,0:T(8,128)(2,1)}, u32[]{:S(2)}, u32[]{:S(2)}) %collective-permute-start.14) | collective-permute-done | bytes 2359328 | tf_op jit(solution)/shard_map/ppermute | solution.py:666
  1390.1 48.5 %collective-permute-done.18.refs_2_ = bf16[4,384,768]{2,1,0:T(8,128)(2,1)} collective-permute-done((bf16[4,384,768]{2,1,0:T(8,128)(2,1)}, bf16[4,384,768]{2,1,0:T(8,128)(2,1)}, u32[]{:S(2)}, u32[]{:S(2)}) %collective-permute-start.18) | collective-permute-done | bytes 2359328 | tf_op jit(solution)/shard_map/ppermute | solution.py:666
  1440.7 48.4 %collective-permute-done.22.refs_7_ = bf16[4,384,768]{2,1,0:T(8,128)(2,1)S(1)} collective-permute-done((bf16[4,384,768]{2,1,0:T(8,128)(2,1)}, bf16[4,384,768]{2,1,0:T(8,128)(2,1)S(1)}, u32[]{:S(2)}, u32[]{:S(2)}) %collective-permute-start.22) | collective-permute-done | bytes 2359328 | tf_op jit(solution)/shard_map/ppermute | solution.py:666
  1491.2 33.3 %shard_map.189 = (bf16[1024,3072]{1,0:T(8,128)(2,1)}, bf16[1024,768]{1,0:T(8,128)(2,1)}, bf16[1024,768]{1,0:T(8,128)(2,1)}, bf16[1024,3072]{1,0:T(8,128)(2,1)}, f32[16,768]{1,0:T(8,128)}) custom-call(s32[4,2]{1,0:T(4,128)} %pad_add_fusion.flags_ref, bf16[1024,768]{1,0:T(8,128)(2,1)} %get-tuple-element.212.dh2_ref.refs_1_, ...), custom_call_target="tpu_custom_call" | custom-call | flops 15703474176 | bytes 31457280 | tf_op jit(solution)/shard_map/pallas_call | solution.py:368
  1524.5 25.1 %shard_map.190.refs_1_ = bf16[8,384,768]{2,1,0:T(8,128)(2,1)} custom-call(bf16[1024,3072]{1,0:T(8,128)(2,1)} %get-tuple-element.214.refs_0_, bf16[1024,768]{1,0:T(8,128)(2,1)} %get-tuple-element.212.dh2_ref.refs_1_, bf16[4,1024,768]{2,1,0:T(8,128)(2,1)} %get-tuple-element.184.a2_ref.refs_2_, bf16[1024,3072]{1,0:T(8,128)(2,1)} %get-tuple-element.215.refs_3_), custom_call_target="tpu_custom_call" | custom-call | flops 9663676416 | bytes 18874368 | tf_op jit(solution)/shard_map/pallas_call | solution.py:495
  1549.6 91.3 %collective-permute-done.20.refs_3_ = bf16[4,384,768]{2,1,0:T(8,128)(2,1)} collective-permute-done((bf16[4,384,768]{2,1,0:T(8,128)(2,1)}, bf16[4,384,768]{2,1,0:T(8,128)(2,1)}, u32[]{:S(2)}, u32[]{:S(2)}) %collective-permute-start.20) | collective-permute-done | bytes 2359328 | tf_op jit(solution)/shard_map/ppermute | solution.py:666
  1642.9 48.5 %collective-permute-done.21.refs_6_ = bf16[4,384,768]{2,1,0:T(8,128)(2,1)} collective-permute-done((bf16[4,384,768]{2,1,0:T(8,128)(2,1)}, bf16[4,384,768]{2,1,0:T(8,128)(2,1)}, u32[]{:S(2)}, u32[]{:S(2)}) %collective-permute-start.21) | collective-permute-done | bytes 2359328 | tf_op jit(solution)/shard_map/ppermute | solution.py:666
  1696.2 34.1 %attn_bwd.15 = (bf16[1024,2304]{1,0:T(8,128)(2,1)}, f32[3,16,768]{2,1,0:T(8,128)}) custom-call(bf16[4,1024,2304]{2,1,0:T(8,128)(2,1)} %get-tuple-element.183.q_ref.k_ref.v_ref, bf16[4,1024,2304]{2,1,0:T(8,128)(2,1)} %get-tuple-element.183.q_ref.k_ref.v_ref, bf16[4,1024,2304]{2,1,0:T(8,128)(2,1)} %get-tuple-element.183.q_ref.k_ref.v_ref, ...), custom_call_target="tpu_custom_call" | custom-call | flops 12884901888 | bytes 12582912 | tf_op jit(solution)/shard_map/attn_bwd/pallas_call | solution.py:348
  1730.4 15.6 shard_map.191.refs_1_
  1773.6 372.7 %collective-permute-done.19.refs_2_ = bf16[4,384,768]{2,1,0:T(8,128)(2,1)} collective-permute-done((bf16[4,384,768]{2,1,0:T(8,128)(2,1)S(1)}, bf16[4,384,768]{2,1,0:T(8,128)(2,1)}, u32[]{:S(2)}, u32[]{:S(2)}) %collective-permute-start.19) | collective-permute-done | bytes 2359328 | tf_op jit(solution)/shard_map/ppermute | solution.py:666
  2228.9 14.5 final_total.12
  2260.0 14.5 final_total.13
  2274.5 35.6 %collective-permute-done.28.refs_3_ = bf16[4,384,768]{2,1,0:T(8,128)(2,1)} collective-permute-done((bf16[4,384,768]{2,1,0:T(8,128)(2,1)}, bf16[4,384,768]{2,1,0:T(8,128)(2,1)}, u32[]{:S(2)}, u32[]{:S(2)}) %collective-permute-start.28) | collective-permute-done | bytes 2359328 | tf_op jit(solution)/shard_map/ppermute | solution.py:666
  2310.1 50.6 %collective-permute-done.30.refs_7_ = bf16[4,384,768]{2,1,0:T(8,128)(2,1)} collective-permute-done((bf16[4,384,768]{2,1,0:T(8,128)(2,1)}, bf16[4,384,768]{2,1,0:T(8,128)(2,1)}, u32[]{:S(2)}, u32[]{:S(2)}) %collective-permute-start.30) | collective-permute-done | bytes 2359328 | tf_op jit(solution)/shard_map/ppermute | solution.py:666
  2360.7 50.6 %collective-permute-done.27.refs_2_ = bf16[4,384,768]{2,1,0:T(8,128)(2,1)} collective-permute-done((bf16[4,384,768]{2,1,0:T(8,128)(2,1)}, bf16[4,384,768]{2,1,0:T(8,128)(2,1)}, u32[]{:S(2)}, u32[]{:S(2)}) %collective-permute-start.27) | collective-permute-done | bytes 2359328 | tf_op jit(solution)/shard_map/ppermute | solution.py:666
  2411.2 49.8 %collective-permute-done.29.refs_6_ = bf16[4,384,768]{2,1,0:T(8,128)(2,1)} collective-permute-done((bf16[4,384,768]{2,1,0:T(8,128)(2,1)S(1)}, bf16[4,384,768]{2,1,0:T(8,128)(2,1)}, u32[]{:S(2)}, u32[]{:S(2)}) %collective-permute-start.29) | collective-permute-done | bytes 2359328 | tf_op jit(solution)/shard_map/ppermute | solution.py:666
  (195 shorter events, 284.0 us)
Async XLA Ops:
  0.6 57.6 %copy-start.3 = (bf16[1,2,1024,768]{3,2,1,0:T(8,128)(2,1)S(1)}, bf16[1,2,1024,768]{3,2,1,0:T(8,128)(2,1)}, u32[]{:S(2)}) copy-start(bf16[1,2,1024,768]{3,2,1,0:T(8,128)(2,1)} %param.9) | copy-start | bytes 9437188
  0.7 61.1 %collective-permute-start.4 = (bf16[2,768,3072]{2,1,0:T(8,128)(2,1)}, bf16[2,768,3072]{2,1,0:T(8,128)(2,1)}, u32[]{:S(2)}, u32[]{:S(2)}) collective-permute-start(bf16[2,768,3072]{2,1,0:T(8,128)(2,1)} %bitcast.166), channel_id=1, source_target_pairs={{0,1},{1,0},{2,3},{3,2},{4,5},{5,4},{6,7},{7,6}} | collective-permute-start | bytes 28311560 | tf_op jit(solution)/shard_map/ppermute | solution.py:631
  1.5 61.6 %collective-permute-start.5 = (bf16[2,3072,768]{2,1,0:T(8,128)(2,1)}, bf16[2,3072,768]{2,1,0:T(8,128)(2,1)}, u32[]{:S(2)}, u32[]{:S(2)}) collective-permute-start(bf16[2,3072,768]{2,1,0:T(8,128)(2,1)} %bitcast.177), channel_id=1, source_target_pairs={{0,1},{1,0},{2,3},{3,2},{4,5},{5,4},{6,7},{7,6}} | collective-permute-start | bytes 28311560 | tf_op jit(solution)/shard_map/ppermute | solution.py:631
  1.5 61.6 %collective-permute-start.2 = (bf16[2,2304,768]{2,1,0:T(8,128)(2,1)}, bf16[2,2304,768]{2,1,0:T(8,128)(2,1)}, u32[]{:S(2)}, u32[]{:S(2)}) collective-permute-start(bf16[2,2304,768]{2,1,0:T(8,128)(2,1)} %bitcast.129), channel_id=1, source_target_pairs={{0,1},{1,0},{2,3},{3,2},{4,5},{5,4},{6,7},{7,6}} | collective-permute-start | bytes 21233672 | tf_op jit(solution)/shard_map/ppermute | solution.py:631
  2.0 61.1 %collective-permute-start.3 = (bf16[2,768,768]{2,1,0:T(8,128)(2,1)}, bf16[2,768,768]{2,1,0:T(8,128)(2,1)}, u32[]{:S(2)}, u32[]{:S(2)}) collective-permute-start(bf16[2,768,768]{2,1,0:T(8,128)(2,1)} %bitcast.188), channel_id=1, source_target_pairs={{0,1},{1,0},{2,3},{3,2},{4,5},{5,4},{6,7},{7,6}} | collective-permute-start | bytes 7077896 | tf_op jit(solution)/shard_map/ppermute | solution.py:631
  3.6 39.5 %collective-permute-start.1 = (bf16[2,9984]{1,0:T(2,128)(2,1)S(1)}, bf16[2,9984]{1,0:T(2,128)(2,1)S(1)}, u32[]{:S(2)}, u32[]{:S(2)}) collective-permute-start(bf16[2,9984]{1,0:T(2,128)(2,1)S(1)} %pad_maximum_fusion), channel_id=1, source_target_pairs={{0,1},{1,0},{2,3},{3,2},{4,5},{5,4},{6,7},{7,6}} | collective-permute-start | bytes 119816 | tf_op jit(solution)/shard_map/ppermute | solution.py:631
  43.1 15.1 collective-permute-start
  63.0 178.8 %collective-permute-start.6 = (bf16[1024,768]{1,0:T(8,128)(2,1)}, bf16[1024,768]{1,0:T(8,128)(2,1)}, u32[]{:S(2)}, u32[]{:S(2)}) collective-permute-start(bf16[1024,768]{1,0:T(8,128)(2,1)} %dynamic-slice_bitcast_fusion), channel_id=1, source_target_pairs={{0,1},{1,0},{2,3},{3,2},{4,5},{5,4},{6,7},{7,6}} | collective-permute-start | bytes 4718600 | tf_op jit(solution)/shard_map/ppermute | solution.py:631
  63.1 178.7 %copy-start.5 = (bf16[1,2,1024,768]{3,2,1,0:T(8,128)(2,1)S(1)}, bf16[1,2,1024,768]{3,2,1,0:T(8,128)(2,1)}, u32[]{:S(2)}) copy-start(bf16[1,2,1024,768]{3,2,1,0:T(8,128)(2,1)} %param.10) | copy-start | bytes 9437188
  1130.7 562.8 %collective-permute-start.17 = (bf16[8,384,768]{2,1,0:T(8,128)(2,1)}, bf16[8,384,768]{2,1,0:T(8,128)(2,1)}, u32[]{:S(2)}, u32[]{:S(2)}) collective-permute-start(bf16[8,384,768]{2,1,0:T(8,128)(2,1)} %shard_map.182.refs_5_), channel_id=1, source_target_pairs={{0,2},{1,3},{2,0},{3,1},{4,6},{5,7},{6,4},{7,5}} | collective-permute-start | bytes 14155784 | tf_op jit(solution)/shard_map/ppermute | solution.py:666
  1133.5 560.1 %collective-permute-start.15 = (bf16[8,384,768]{2,1,0:T(8,128)(2,1)}, bf16[8,384,768]{2,1,0:T(8,128)(2,1)}, u32[]{:S(2)}, u32[]{:S(2)}) collective-permute-start(bf16[8,384,768]{2,1,0:T(8,128)(2,1)} %shard_map.178.refs_1_), channel_id=1, source_target_pairs={{0,2},{1,3},{2,0},{3,1},{4,6},{5,7},{6,4},{7,5}} | collective-permute-start | bytes 14155784 | tf_op jit(solution)/shard_map/ppermute | solution.py:666
  1133.5 254.6 %collective-permute-start.14 = (bf16[4,384,768]{2,1,0:T(8,128)(2,1)}, bf16[4,384,768]{2,1,0:T(8,128)(2,1)}, u32[]{:S(2)}, u32[]{:S(2)}) collective-permute-start(bf16[4,384,768]{2,1,0:T(8,128)(2,1)} %shard_map.160.refs_0_), channel_id=1, source_target_pairs={{0,2},{1,3},{2,0},{3,1},{4,6},{5,7},{6,4},{7,5}} | collective-permute-start | bytes 7077896 | tf_op jit(solution)/shard_map/ppermute | solution.py:666
  1135.5 303.2 %collective-permute-start.18 = (bf16[4,384,768]{2,1,0:T(8,128)(2,1)}, bf16[4,384,768]{2,1,0:T(8,128)(2,1)}, u32[]{:S(2)}, u32[]{:S(2)}) collective-permute-start(bf16[4,384,768]{2,1,0:T(8,128)(2,1)} %shard_map.162.refs_0_), channel_id=1, source_target_pairs={{0,2},{1,3},{2,0},{3,1},{4,6},{5,7},{6,4},{7,5}} | collective-permute-start | bytes 7077896 | tf_op jit(solution)/shard_map/ppermute | solution.py:666
  1135.5 353.6 %collective-permute-start.22 = (bf16[4,384,768]{2,1,0:T(8,128)(2,1)}, bf16[4,384,768]{2,1,0:T(8,128)(2,1)S(1)}, u32[]{:S(2)}, u32[]{:S(2)}) collective-permute-start(bf16[4,384,768]{2,1,0:T(8,128)(2,1)} %shard_map.183.refs_5_), channel_id=1, source_target_pairs={{0,2},{1,3},{2,0},{3,1},{4,6},{5,7},{6,4},{7,5}} | collective-permute-start | bytes 7077896 | tf_op jit(solution)/shard_map/ppermute | solution.py:666
  1388.1 307.4 %collective-permute-start.16 = (bf16[8,384,768]{2,1,0:T(8,128)(2,1)}, bf16[8,384,768]{2,1,0:T(8,128)(2,1)}, u32[]{:S(2)}, u32[]{:S(2)}) collective-permute-start(bf16[8,384,768]{2,1,0:T(8,128)(2,1)} %shard_map.166.refs_4_), channel_id=1, source_target_pairs={{0,2},{1,3},{2,0},{3,1},{4,6},{5,7},{6,4},{7,5}} | collective-permute-start | bytes 14155784 | tf_op jit(solution)/shard_map/ppermute | solution.py:666
  1438.7 202.2 %collective-permute-start.20 = (bf16[4,384,768]{2,1,0:T(8,128)(2,1)}, bf16[4,384,768]{2,1,0:T(8,128)(2,1)}, u32[]{:S(2)}, u32[]{:S(2)}) collective-permute-start(bf16[4,384,768]{2,1,0:T(8,128)(2,1)} %shard_map.179.refs_1_), channel_id=1, source_target_pairs={{0,2},{1,3},{2,0},{3,1},{4,6},{5,7},{6,4},{7,5}} | collective-permute-start | bytes 7077896 | tf_op jit(solution)/shard_map/ppermute | solution.py:666
  1489.1 35.3 %copy-start.2 = (bf16[4,384,768]{2,1,0:T(8,128)(2,1)}, bf16[4,384,768]{2,1,0:T(8,128)(2,1)S(1)}, u32[]{:S(2)}) copy-start(bf16[4,384,768]{2,1,0:T(8,128)(2,1)S(1)} %collective-permute-done.22.refs_7_) | copy-start | bytes 7077892
  1489.1 202.3 %collective-permute-start.21 = (bf16[4,384,768]{2,1,0:T(8,128)(2,1)}, bf16[4,384,768]{2,1,0:T(8,128)(2,1)}, u32[]{:S(2)}, u32[]{:S(2)}) collective-permute-start(bf16[4,384,768]{2,1,0:T(8,128)(2,1)} %shard_map.167.refs_4_), channel_id=1, source_target_pairs={{0,2},{1,3},{2,0},{3,1},{4,6},{5,7},{6,4},{7,5}} | collective-permute-start | bytes 7077896 | tf_op jit(solution)/shard_map/ppermute | solution.py:666
  1524.4 171.1 %copy-start = (bf16[4,384,768]{2,1,0:T(8,128)(2,1)S(1)}, bf16[4,384,768]{2,1,0:T(8,128)(2,1)}, u32[]{:S(2)}) copy-start(bf16[4,384,768]{2,1,0:T(8,128)(2,1)} %shard_map.163.refs_0_) | copy-start | bytes 7077892
  1640.9 513.2 %collective-permute-start.10 = (bf16[8,384,768]{2,1,0:T(8,128)(2,1)}, bf16[8,384,768]{2,1,0:T(8,128)(2,1)}, u32[]{:S(2)}, u32[]{:S(2)}) collective-permute-start(bf16[8,384,768]{2,1,0:T(8,128)(2,1)} %shard_map.190.refs_1_), channel_id=1, source_target_pairs={{0,2},{1,3},{2,0},{3,1},{4,6},{5,7},{6,4},{7,5}} | collective-permute-start | bytes 14155784 | tf_op jit(solution)/shard_map/ppermute | solution.py:666
  1691.5 463.2 %collective-permute-start.12 = (bf16[8,384,768]{2,1,0:T(8,128)(2,1)}, bf16[8,384,768]{2,1,0:T(8,128)(2,1)}, u32[]{:S(2)}, u32[]{:S(2)}) collective-permute-start(bf16[8,384,768]{2,1,0:T(8,128)(2,1)} %shard_map.186.refs_5_), channel_id=1, source_target_pairs={{0,2},{1,3},{2,0},{3,1},{4,6},{5,7},{6,4},{7,5}} | collective-permute-start | bytes 14155784 | tf_op jit(solution)/shard_map/ppermute | solution.py:666
  1693.5 461.9 %collective-permute-start.9 = (bf16[8,384,768]{2,1,0:T(8,128)(2,1)}, bf16[8,384,768]{2,1,0:T(8,128)(2,1)}, u32[]{:S(2)}, u32[]{:S(2)}) collective-permute-start(bf16[8,384,768]{2,1,0:T(8,128)(2,1)} %shard_map.174.refs_0_), channel_id=1, source_target_pairs={{0,2},{1,3},{2,0},{3,1},{4,6},{5,7},{6,4},{7,5}} | collective-permute-start | bytes 14155784 | tf_op jit(solution)/shard_map/ppermute | solution.py:666
  1693.5 461.9 %collective-permute-start.11 = (bf16[8,384,768]{2,1,0:T(8,128)(2,1)}, bf16[8,384,768]{2,1,0:T(8,128)(2,1)}, u32[]{:S(2)}, u32[]{:S(2)}) collective-permute-start(bf16[8,384,768]{2,1,0:T(8,128)(2,1)} %shard_map.170.refs_4_), channel_id=1, source_target_pairs={{0,2},{1,3},{2,0},{3,1},{4,6},{5,7},{6,4},{7,5}} | collective-permute-start | bytes 14155784 | tf_op jit(solution)/shard_map/ppermute | solution.py:666
  1695.5 450.8 %collective-permute-start.19 = (bf16[4,384,768]{2,1,0:T(8,128)(2,1)S(1)}, bf16[4,384,768]{2,1,0:T(8,128)(2,1)}, u32[]{:S(2)}, u32[]{:S(2)}) collective-permute-start(bf16[4,384,768]{2,1,0:T(8,128)(2,1)S(1)} %copy-done), channel_id=1, source_target_pairs={{0,2},{1,3},{2,0},{3,1},{4,6},{5,7},{6,4},{7,5}} | collective-permute-start | bytes 7077896 | tf_op jit(solution)/shard_map/ppermute | solution.py:666
  2146.3 53.5 %collective-permute-start.25 = (f32[4,384,768]{2,1,0:T(8,128)}, f32[4,384,768]{2,1,0:T(8,128)}, u32[]{:S(2)}, u32[]{:S(2)}) collective-permute-start(f32[4,384,768]{2,1,0:T(8,128)} %send_total.7), channel_id=1, source_target_pairs={{0,1},{1,0},{2,3},{3,2},{4,5},{5,4},{6,7},{7,6}} | collective-permute-start | bytes 14155784 | tf_op jit(solution)/shard_map/ppermute | solution.py:631
  2154.2 60.2 %collective-permute-start.24 = (f32[4,384,768]{2,1,0:T(8,128)}, f32[4,384,768]{2,1,0:T(8,128)}, u32[]{:S(2)}, u32[]{:S(2)}) collective-permute-start(f32[4,384,768]{2,1,0:T(8,128)} %send_total.8), channel_id=1, source_target_pairs={{0,1},{1,0},{2,3},{3,2},{4,5},{5,4},{6,7},{7,6}} | collective-permute-start | bytes 14155784 | tf_op jit(solution)/shard_map/ppermute | solution.py:631
  2154.7 28.7 %collective-permute-start.23 = (f32[4,384,768]{2,1,0:T(8,128)}, f32[4,384,768]{2,1,0:T(8,128)}, u32[]{:S(2)}, u32[]{:S(2)}) collective-permute-start(f32[4,384,768]{2,1,0:T(8,128)} %send_total.9), channel_id=1, source_target_pairs={{0,1},{1,0},{2,3},{3,2},{4,5},{5,4},{6,7},{7,6}} | collective-permute-start | bytes 14155784 | tf_op jit(solution)/shard_map/ppermute | solution.py:631
  2155.4 10.3 copy-start.15
  2155.4 12.1 copy-start.14
  2155.4 13.9 copy-start.13
  2155.4 15.7 copy-start.12
  2155.4 17.5 copy-start.11
  2155.4 19.3 copy-start.10
  2155.4 21.1 copy-start.9
  2155.4 22.9 copy-start.8
  2163.4 65.4 %collective-permute-start.13 = (f32[4,384,768]{2,1,0:T(8,128)}, f32[4,384,768]{2,1,0:T(8,128)}, u32[]{:S(2)}, u32[]{:S(2)}) collective-permute-start(f32[4,384,768]{2,1,0:T(8,128)} %send_total.6), channel_id=1, source_target_pairs={{0,1},{1,0},{2,3},{3,2},{4,5},{5,4},{6,7},{7,6}} | collective-permute-start | bytes 14155784 | tf_op jit(solution)/shard_map/ppermute | solution.py:631
  2178.9 72.3 %collective-permute-start.32 = (f32[8,9984]{1,0:T(8,128)S(1)}, f32[8,9984]{1,0:T(8,128)S(1)}, u32[]{:S(2)}, u32[]{:S(2)}) collective-permute-start(f32[8,9984]{1,0:T(8,128)S(1)} %stack.198), channel_id=1, source_target_pairs={{0,1},{1,0},{2,3},{3,2},{4,5},{5,4},{6,7},{7,6}} | collective-permute-start | bytes 958472 | tf_op jit(solution)/shard_map/ppermute | solution.py:631
  2251.2 7.1 copy-start.1
  2251.2 8.7 collective-permute-start.26
  2251.3 7.0 collective-permute-start.33
  2255.7 54.4 %collective-permute-start.28 = (bf16[4,384,768]{2,1,0:T(8,128)(2,1)}, bf16[4,384,768]{2,1,0:T(8,128)(2,1)}, u32[]{:S(2)}, u32[]{:S(2)}) collective-permute-start(bf16[4,384,768]{2,1,0:T(8,128)(2,1)} %shard_map.191.refs_1_), channel_id=1, source_target_pairs={{0,2},{1,3},{2,0},{3,1},{4,6},{5,7},{6,4},{7,5}} | collective-permute-start | bytes 7077896 | tf_op jit(solution)/shard_map/ppermute | solution.py:666
  2256.3 104.4 %collective-permute-start.30 = (bf16[4,384,768]{2,1,0:T(8,128)(2,1)}, bf16[4,384,768]{2,1,0:T(8,128)(2,1)}, u32[]{:S(2)}, u32[]{:S(2)}) collective-permute-start(bf16[4,384,768]{2,1,0:T(8,128)(2,1)} %shard_map.187.refs_5_), channel_id=1, source_target_pairs={{0,2},{1,3},{2,0},{3,1},{4,6},{5,7},{6,4},{7,5}} | collective-permute-start | bytes 7077896 | tf_op jit(solution)/shard_map/ppermute | solution.py:666
  2257.7 153.5 %collective-permute-start.27 = (bf16[4,384,768]{2,1,0:T(8,128)(2,1)}, bf16[4,384,768]{2,1,0:T(8,128)(2,1)}, u32[]{:S(2)}, u32[]{:S(2)}) collective-permute-start(bf16[4,384,768]{2,1,0:T(8,128)(2,1)} %shard_map.175.refs_0_), channel_id=1, source_target_pairs={{0,2},{1,3},{2,0},{3,1},{4,6},{5,7},{6,4},{7,5}} | collective-permute-start | bytes 7077896 | tf_op jit(solution)/shard_map/ppermute | solution.py:666
  2258.3 202.7 %collective-permute-start.29 = (bf16[4,384,768]{2,1,0:T(8,128)(2,1)S(1)}, bf16[4,384,768]{2,1,0:T(8,128)(2,1)}, u32[]{:S(2)}, u32[]{:S(2)}) collective-permute-start(bf16[4,384,768]{2,1,0:T(8,128)(2,1)S(1)} %copy-done.1), channel_id=1, source_target_pairs={{0,2},{1,3},{2,0},{3,1},{4,6},{5,7},{6,4},{7,5}} | collective-permute-start | bytes 7077896 | tf_op jit(solution)/shard_map/ppermute | solution.py:666
  2259.9 211.4 %collective-permute-start.8 = (bf16[1024,768]{1,0:T(8,128)(2,1)}, bf16[1024,768]{1,0:T(8,128)(2,1)}, u32[]{:S(2)}, u32[]{:S(2)}) collective-permute-start(bf16[1024,768]{1,0:T(8,128)(2,1)} %broadcast_select_fusion), channel_id=1, source_target_pairs={{0,1},{1,0},{2,3},{3,2},{4,5},{5,4},{6,7},{7,6}} | collective-permute-start | bytes 4718600 | tf_op jit(solution)/shard_map/ppermute | solution.py:631
  2310.1 166.4 %collective-permute-start.7 = (bf16[1024,768]{1,0:T(8,128)(2,1)}, bf16[1024,768]{1,0:T(8,128)(2,1)}, u32[]{:S(2)}, u32[]{:S(2)}) collective-permute-start(bf16[1024,768]{1,0:T(8,128)(2,1)} %get-tuple-element.294), channel_id=1, source_target_pairs={{0,1},{1,0},{2,3},{3,2},{4,5},{5,4},{6,7},{7,6}} | collective-permute-start | bytes 4718600 | tf_op jit(solution)/shard_map/ppermute | solution.py:631
  2469.1 11.2 collective-permute-start.31
  2471.4 5.1 copy-start.7
  (2 other events, 8.6 us)
